TPU v7x, 32 devices: a whole 2x2x4 slice. The times are simulated.
32 devices in a mesh: dp: 8 (over z, x), tensor: 4 (over y, core).
Axes of the slice: x: 2, y: 2, z: 4, core: 2. Of those that a mesh axis runs over, the one named last changes fastest.
Arguments:
- out_grad: bfloat16 [1536, 2048], P(('dp', 'tensor')), may hold values from -6 to 6
- gate_pre: bfloat16 [1536, 7168], P('dp', 'tensor'), may hold values from -6 to 6
- up_pre: bfloat16 [1536, 7168], P('dp', 'tensor'), may hold values from -6 to 6
- down_weight: bfloat16 [7168, 2048], P('tensor', 'dp'), may hold values from -0.0625 to 0.0625
- up_weight: bfloat16 [2048, 7168], P('dp', 'tensor'), may hold values from -0.125 to 0.125
Outputs:
- input_grad: bfloat16 [1536, 2048], P(('dp', 'tensor'))
- gate_grad: bfloat16 [1536, 7168], P('dp', 'tensor')
- down_grad_t: float32 [2048, 7168], P('dp', 'tensor')
All inputs are finite; a program needn't handle non-finite values.
Results may differ from a plain program's by a relative error of at most 0.009.
Values may be sent and summed in bfloat16 or wider, within the bound.
No kernel may reach another device: no remote copies, remote signals or barrier semaphores. Data moves between devices by JAX's collectives and lax.ppermute only.
A program may use at most 128 MiB of HBM per device.

v0:
```python
import jax
import jax.numpy as jnp
from jax import lax
from jax.sharding import PartitionSpec as P


def shards(out_grad, gate_pre, up_pre, down_weight, up_weight):
    grad_rows = lax.all_gather(out_grad, "tensor", axis=0, tiled=True)
    gate_f = gate_pre.astype(jnp.float32)
    up_f = up_pre.astype(jnp.float32)
    sigmoid_gate = jax.nn.sigmoid(gate_f)
    swish_gate = gate_f * sigmoid_gate
    hidden = (swish_gate * up_f).astype(jnp.bfloat16)
    contract = (((1,), (1,)), ((), ()))
    whole_down, whole_up = (
        lax.all_gather(down_weight, "dp", axis=1, tiled=True),
        lax.all_gather(up_weight, "dp", axis=0, tiled=True),
    )
    upstream = lax.dot_general(grad_rows, whole_down, contract, preferred_element_type=jnp.float32)
    gate_grad = (upstream * up_f * sigmoid_gate * (1.0 + gate_f * (1.0 - sigmoid_gate))).astype(
        jnp.bfloat16
    )
    up_grad = (upstream * swish_gate).astype(jnp.bfloat16)
    replicas = lax.axis_size("dp")
    partial_sum = lax.dot_general(up_grad, whole_up, contract, preferred_element_type=jnp.float32)
    input_grad = lax.psum_scatter(
        partial_sum.astype(jnp.bfloat16), "tensor", scatter_dimension=0, tiled=True
    )
    product = lax.dot_general(
        grad_rows, hidden, (((0,), (0,)), ((), ())), preferred_element_type=jnp.float32
    )
    down_grad = lax.psum_scatter(product / replicas, "dp", scatter_dimension=0, tiled=True)
    return (input_grad, gate_grad, down_grad)


def solution(mesh):
    placed = (
        P(("dp", "tensor"), None),
        P("dp", "tensor"),
        P("dp", "tensor"),
        P("tensor", "dp"),
        P("dp", "tensor"),
    )
    return jax.shard_map(
        shards,
        mesh=mesh,
        in_specs=placed,
        out_specs=(P(("dp", "tensor"), None), P("dp", "tensor"), P("dp", "tensor")),
        check_vma=False,
    )
```

profile of v0, /device:TPU:0, one launch (start us, length us, event | category | flops | bytes accessed | tf_op | source)
XLA Modules:
  0.0 507.6 jit_solution(8489506215518296360)
XLA Ops:
  7.2 0.0 copy-start.2
  7.2 0.0 copy-start.1
  7.2 0.0 copy-start
  7.2 0.0 all-gather.3.cloned.1.call-start
  7.2 0.7 all-gather.3.cloned.1.call-update
  7.9 0.0 all-gather.5.cloned.1.call-start
  8.0 0.7 all-gather.5.cloned.1.call-update
  8.7 0.0 reduce-scatter.5.cloned.1.call-start
  8.7 0.0 copy-done.2
  8.7 10.1 %all_gather.9 = bf16[192,2048]{1,0:T(8,128)(2,1)S(1)} all-gather(bf16[48,2048]{1,0:T(8,128)(2,1)S(1)} %copy-done.2), channel_id=1, replica_groups=mesh['dp'=8,'tensor'=4] {'tensor'}, dimensions={0}, use_global_device_ids=true | all-gather | bytes 983040 | tf_op jit(solution)/shard_map/all_gather | solution.py:8
  18.8 0.0 copy-done.1
  18.8 0.0 copy-done
  18.8 7.4 %multiply_bitcast_fusion = f32[2048,1792]{0,1:T(8,128)} fusion(bf16[192,2048]{1,0:T(8,128)(2,1)S(1)} %all_gather.9, bf16[192,1792]{1,0:T(8,128)(2,1)S(1)} %copy-done, bf16[192,1792]{1,0:T(8,128)(2,1)S(1)} %copy-done.1), kind=kOutput, calls=%fused_computation | convolution fusion | flops 1415708672 | bytes 16842752 | tf_op jit(solution)/shard_map/dot_general | solution.py:29
  26.2 0.0 reduce-scatter.5.cloned.1.call-update
  26.2 0.0 reduce-scatter.3.cloned.1.call-start
  26.3 98.7 %all-gather.3.cloned.1.call-done = bf16[1792,2048]{1,0:T(8,128)(2,1)} async-done(((bf16[1792,256]{1,0:T(8,128)(2,1)}), bf16[1792,2048]{1,0:T(8,128)(2,1)}) %all-gather.3.cloned.1.call-update) | async-done | bytes 7340048 | tf_op jit(solution)/shard_map/all_gather | solution.py:16
  125.0 7.1 %fusion.2 = (bf16[192,1792]{1,0:T(8,128)(2,1)}, f32[192,1792]{1,0:T(8,128)}) fusion(bf16[192,1792]{1,0:T(8,128)(2,1)S(1)} %copy-done, bf16[192,1792]{1,0:T(8,128)(2,1)S(1)} %copy-done.1, bf16[192,2048]{1,0:T(8,128)(2,1)S(1)} %all_gather.9, bf16[1792,2048]{1,0:T(8,128)(2,1)} %all-gather.3.cloned.1.call-done), kind=kOutput, calls=%fused_computation.9 | convolution fusion | flops 1413414912 | bytes 11567104 | tf_op jit(solution)/shard_map/dot_general | solution.py:19
  132.1 104.8 %all-gather.5.cloned.1.call-done = bf16[2048,1792]{1,0:T(8,128)(2,1)} async-done(((bf16[256,1792]{1,0:T(8,128)(2,1)}), bf16[2048,1792]{1,0:T(8,128)(2,1)}) %all-gather.5.cloned.1.call-update) | async-done | bytes 7340048 | tf_op jit(solution)/shard_map/all_gather | solution.py:17
  236.9 7.0 %convolution_convert_fusion = bf16[192,2048]{1,0:T(8,128)(2,1)} fusion(bf16[2048,1792]{1,0:T(8,128)(2,1)} %all-gather.5.cloned.1.call-done, f32[192,1792]{1,0:T(8,128)} %get-tuple-element.7, bf16[192,1792]{1,0:T(8,128)(2,1)S(1)} %copy-done.1), kind=kOutput, calls=%fused_computation.1 | convolution fusion | flops 1412087808 | bytes 10190848 | tf_op jit(solution)/shard_map/dot_general | solution.py:25
  243.8 0.0 reduce-scatter.3.cloned.1.call-update
  243.8 231.9 %reduce-scatter.5.cloned.1.call-done = f32[256,1792]{0,1:T(8,128)} async-done(((f32[2048,1792]{0,1:T(8,128)}), f32[256,1792]{0,1:T(8,128)}) %reduce-scatter.5.cloned.1.call-update) | async-done | bytes 1835024 | tf_op jit(solution)/shard_map/reduce_scatter | solution.py:32
  475.7 2.7 copy.8
  478.5 22.6 %reduce-scatter.3.cloned.1.call-done = bf16[48,2048]{1,0:T(8,128)(2,1)} async-done(((bf16[192,2048]{1,0:T(8,128)(2,1)}), bf16[48,2048]{1,0:T(8,128)(2,1)}) %reduce-scatter.3.cloned.1.call-update) | async-done | bytes 196624 | tf_op jit(solution)/shard_map/reduce_scatter | solution.py:26
Async XLA Ops:
  7.2 1.6 copy-start.2
  7.2 11.7 %copy-start.1 = (bf16[192,1792]{1,0:T(8,128)(2,1)S(1)}, bf16[192,1792]{1,0:T(8,128)(2,1)}, u32[]{:S(2)}) copy-start(bf16[192,1792]{1,0:T(8,128)(2,1)} %param.6) | copy-start | bytes 2064388
  7.2 11.7 %copy-start = (bf16[192,1792]{1,0:T(8,128)(2,1)S(1)}, bf16[192,1792]{1,0:T(8,128)(2,1)}, u32[]{:S(2)}) copy-start(bf16[192,1792]{1,0:T(8,128)(2,1)} %param.7) | copy-start | bytes 2064388
  7.2 117.8 %all-gather.3.cloned.1.call-start = ((), (), s32[]{:S(2)}) async-start(), calls=%async_computation.2 | async-start | bytes 8257536 | tf_op jit(solution)/shard_map/all_gather | solution.py:16
  7.9 228.9 %all-gather.5.cloned.1.call-start = ((), (), s32[]{:S(2)}) async-start(), calls=%async_computation.3 | async-start | bytes 8257536 | tf_op jit(solution)/shard_map/all_gather | solution.py:17
  8.7 467.1 %reduce-scatter.5.cloned.1.call-start = ((), (), s32[]{:S(2)}) async-start(), calls=%async_computation.5 | async-start | bytes 16515072 | tf_op jit(solution)/shard_map/reduce_scatter | solution.py:32
  26.2 474.8 %reduce-scatter.3.cloned.1.call-start = ((), (), s32[]{:S(2)}) async-start(), calls=%async_computation.4 | async-start | bytes 983040 | tf_op jit(solution)/shard_map/reduce_scatter | solution.py:26
Sparse Core Ops, SparseCore 0:
  10.0 114.8 all-gather.2
  127.2 109.6 all-gather.4
  240.5 235.2 reduce-scatter.4
  478.7 22.3 reduce-scatter.2
where the time goes:
time: 508 us
  waiting for transfers between devices  459 us (90%)
  matrix products  21.5 us (4%)
  between operations  13.8 us (3%)
  blocking collectives  10.1 us (2%)
    reduce_scatter x1, waiting for transfers between devices, shards(): lax.psum_scatter(product / replicas, 'dp', scatter_dimension=0, tiled=True)  232 us
    all_gather x1, waiting for transfers between devices, shards(): lax.all_gather(up_weight, 'dp', axis=0, tiled=True)  105 us
    all_gather x1, waiting for transfers between devices, shards(): lax.all_gather(down_weight, 'dp', axis=1, tiled=True)  98.7 us
    reduce_scatter x1, waiting for transfers between devices, shards(): lax.psum_scatter(partial_sum.astype(jnp.bfloat16), 'tensor', scatter_dime...  22.6 us
  transfers between devices with their start and end apart: 4, of which 4 were waited for; matrix products, arithmetic and copies ran while one was open for 5% of the time, Pallas kernels for 0%

commit v1 on v0

v1 whole, which is shorter than its diff:
```python
import jax
import jax.numpy as jnp
from jax import lax
from jax.sharding import PartitionSpec as P


COLUMNS = 2
CHUNKS = 2
LONGEST = 4

f32, bf16 = jnp.float32, jnp.bfloat16


def dot(a, b, dims):
    return lax.dot_general(a, b, (dims, ((), ())), preferred_element_type=f32)


def gathered(out_grad, gate_pre, up_pre, down_weight, up_weight):
    grad_rows = lax.all_gather(out_grad, "tensor", axis=0, tiled=True)
    gate_f, up_f = gate_pre.astype(f32), up_pre.astype(f32)
    sigmoid_gate = jax.nn.sigmoid(gate_f)
    swish_gate = gate_f * sigmoid_gate
    hidden = (swish_gate * up_f).astype(bf16)
    whole_down = lax.all_gather(down_weight, "dp", axis=1, tiled=True)
    whole_up = lax.all_gather(up_weight, "dp", axis=0, tiled=True)
    upstream = dot(grad_rows, whole_down, ((1,), (1,)))
    gate_grad = (upstream * up_f * sigmoid_gate * (1.0 + gate_f * (1.0 - sigmoid_gate))).astype(bf16)
    up_grad = (upstream * swish_gate).astype(bf16)
    partial = dot(up_grad, whole_up, ((1,), (1,))).astype(bf16)
    input_grad = lax.psum_scatter(partial, "tensor", scatter_dimension=0, tiled=True)
    product = dot(grad_rows, hidden, ((0,), (0,))) / lax.axis_size("dp")
    down_grad = lax.psum_scatter(product, "dp", scatter_dimension=0, tiled=True)
    return input_grad, gate_grad, down_grad


def shards(out_grad, gate_pre, up_pre, down_weight, up_weight):
    replicas, members = lax.axis_size("dp"), lax.axis_size("tensor")
    lines = replicas // COLUMNS
    place, member = lax.axis_index("dp"), lax.axis_index("tensor")
    spot, column = place // COLUMNS, place % COLUMNS
    own_rows, _ = out_grad.shape
    rows, hidden_units = gate_pre.shape
    share = up_weight.shape[0]
    pair = COLUMNS * share
    width = hidden_units // CHUNKS

    def chunk(a, axis, c):
        return lax.slice_in_dim(a, c * width, (c + 1) * width, axis=axis)

    def at(z, x):
        return z * COLUMNS + x

    def along(a, pairs):
        return lax.ppermute(a, "dp", [(at(i, x), at(j, x)) for i, j in pairs for x in range(COLUMNS)])

    def across(a):
        return lax.ppermute(a, "dp", [(at(z, x), at(z, 1 - x)) for z in range(lines) for x in range(COLUMNS)])

    def turn(a, k):
        return along(a, [(i, (i + k) % lines) for i in range(lines)])

    def swap(a, j):
        return lax.ppermute(a, "tensor", [(t, t ^ j) for t in range(members)])

    def piece(z):
        first = (z % lines) * pair
        return jnp.concatenate(
            [lax.dynamic_slice(out_grad, (0, first + x * share), (own_rows, share)) for x in (column, 1 - column)],
            axis=1,
        )

    other_down = across(down_weight)
    groups = {0: jnp.stack([piece(spot)] + [turn(piece(spot + k), k) for k in range(1, lines)])}
    j = members // 2
    while j:
        for have, value in list(groups.items()):
            groups[have ^ j] = swap(value, j)
        j //= 2
    all_groups = jnp.stack([groups[k] for k in range(members)])
    grads = jnp.stack(
        [lax.dynamic_index_in_dim(all_groups, member ^ t, 0, keepdims=False) for t in range(members)], axis=1
    ).reshape(lines, rows, pair)
    grads_left = lax.optimization_barrier(grads)

    other_up = across(up_weight)

    gate_f, up_f = gate_pre.astype(f32), up_pre.astype(f32)
    hidden = (gate_f * jax.nn.sigmoid(gate_f) * up_f).astype(bf16)
    back, ahead = [hidden], [hidden]
    for step in range(1, lines):
        back.append(along(back[-1], [(i, i + 1) for i in range(step - 1, lines - 1)]))
        ahead.append(along(ahead[-1], [(i + 1, i) for i in range(lines - step)]))

    weight = jnp.concatenate([down_weight, other_down], axis=1)
    gate_grads, up_grads = [], []
    for c in range(CHUNKS):
        w = chunk(weight, 0, c)
        r = l = None
        for step in range(1, lines):
            send_r = dot(grads[step], w, ((1,), (1,)))
            send_l = dot(grads_left[lines - step], w, ((1,), (1,)))
            if r is not None:
                send_r, send_l = send_r + r.astype(f32), send_l + l.astype(f32)
            r = along(send_r.astype(bf16), [(i, i + 1) for i in range(step)])
            l = along(send_l.astype(bf16), [(i, i - 1) for i in range(lines - step, lines)])
        upstream = dot(grads[0], w, ((1,), (1,))) + r.astype(f32) + l.astype(f32)
        g, u = chunk(gate_pre, 1, c).astype(f32), chunk(up_pre, 1, c).astype(f32)
        s = jax.nn.sigmoid(g)
        gate_grads.append((upstream * u * s * (1.0 + g * (1.0 - s))).astype(bf16))
        held = {0: (upstream * (g * s)).astype(bf16)}
        for k in range(1, lines // 2 + 1):
            held[k] = turn(held[k - 1], 1)
            if k < lines - k:
                held[lines - k] = turn(held[(lines - k + 1) % lines], lines - 1)
        up_grads.append(held)
        gate_pre, up_pre, _ = lax.optimization_barrier((gate_pre, up_pre, held[0]))
    gate_grad = jnp.concatenate(gate_grads, axis=1)

    line_hidden = jnp.concatenate([hidden] + [back[k] + ahead[lines - k] for k in range(1, lines)])
    both = grads.reshape(lines * rows, pair)
    mine, other = (
        dot(both[:, i * share : (i + 1) * share], line_hidden, ((0,), (0,))) / replicas for i in (0, 1)
    )
    from_pair = across(other.astype(bf16)).astype(f32)
    down_grad = mine + from_pair

    def product(k):
        return jnp.concatenate(
            [
                sum(dot(up_grads[c][k], chunk(w, 1, c), ((1,), (1,))) for c in range(CHUNKS)).astype(bf16)
                for w in (up_weight, other_up)
            ],
            axis=1,
        )

    done = {}
    for step in range(1, lines // 2 + 1):
        ks = sorted({step, lines - step}) + [0] * (step == 1)
        p = jnp.stack([product(k) for k in ks]).reshape(len(ks), members, own_rows, pair)

        def part_of(t):
            return lax.dynamic_index_in_dim(p, t, 1, keepdims=False)

        total = part_of(member).astype(f32)
        for j in range(1, members):
            total = total + swap(part_of(member ^ j), j).astype(f32)
        total = total.astype(bf16)
        for i, k in enumerate(ks):
            done[k] = turn(total[i], lines - k) if k else total[i]
    done = jnp.stack([done[k] for k in range(lines)])
    parts = []
    for z in range(lines):
        block = lax.dynamic_index_in_dim(done, (z - spot) % lines, 0, keepdims=False)
        first, second = block[:, :share], block[:, share:]
        parts += [jnp.where(column == 0, first, second), jnp.where(column == 0, second, first)]
    return jnp.concatenate(parts, axis=1), gate_grad, down_grad


def solution(mesh):
    placed = (
        P(("dp", "tensor"), None),
        P("dp", "tensor"),
        P("dp", "tensor"),
        P("tensor", "dp"),
        P("dp", "tensor"),
    )
    short = mesh.shape["dp"] <= LONGEST * COLUMNS

    def body(*args):
        return (shards if short else gathered)(*args)

    return jax.shard_map(
        body,
        mesh=mesh,
        in_specs=placed,
        out_specs=(P(("dp", "tensor"), None), P("dp", "tensor"), P("dp", "tensor")),
        check_vma=False,
    )
```

time: 508 us -> 194 us (0.38)
  waiting for transfers between devices: 459 us -> 88.9 us
  starting transfers between devices: 0.16 us -> 76.6 us
  between operations: 13.8 us -> 1.42 us
  blocking collectives: 10.1 us -> 0 us
  other arithmetic: 0 us -> 7.26 us
    reduce_scatter x2 -> x0, waiting for transfers between devices: 255 us -> none  [the longest x1 232 us: shards(): lax.psum_scatter(product / replicas, 'dp', scatter_dimension=0, tiled=True)]
    all_gather x2 -> x0, waiting for transfers between devices: 203 us -> none  [the longest x1 105 us: shards(): lax.all_gather(up_weight, 'dp', axis=0, tiled=True)]
    ppermute x0 -> x42, waiting for transfers between devices: none -> 88.9 us  [the longest x30 68.9 us: along(): lax.ppermute(a, 'dp', [(at(i, x), at(j, x)) for i, j in pairs for x in ra...]
    ppermute x0 -> x42, starting transfers between devices: none -> 76.6 us  [the longest x30 66.5 us: along(): lax.ppermute(a, 'dp', [(at(i, x), at(j, x)) for i, j in pairs for x in ra...]
    all_gather x1 -> x0, blocking collectives: 10.1 us -> none  [shards(): grad_rows = lax.all_gather(out_grad, 'tensor', axis=0, tiled=True)]
    dot_general x3 -> x32, matrix products: 21.5 us -> 17.3 us  [dot(): return lax.dot_general(a, b, (dims, ((), ())), preferred_element_type=f32)]
  transfers between devices with their start and end apart: 4 -> 42, of which waited for: 4 -> 18; matrix products, arithmetic and copies ran while one was open for 5% -> 12% of each run, Pallas kernels for 0% -> 0%
where the time goes in v1:
time: 194 us
  waiting for transfers between devices  88.9 us (46%)
  starting transfers between devices  76.6 us (39%)
  matrix products  17.3 us (9%)
  other arithmetic  7.26 us (4%)
  local copies, waits for them, and re-layouts  2.29 us (1%)
    ppermute x30, waiting for transfers between devices, along(): lax.ppermute(a, 'dp', [(at(i, x), at(j, x)) for i, j in pairs for x in ra...  68.9 us
    ppermute x30, starting transfers between devices, along(): lax.ppermute(a, 'dp', [(at(i, x), at(j, x)) for i, j in pairs for x in ra...  66.5 us
    ppermute x3, waiting for transfers between devices, across(): lax.ppermute(a, 'dp', [(at(z, x), at(z, 1 - x)) for z in range(lines) for...  18.6 us
    dot_general x32, matrix products, dot(): return lax.dot_general(a, b, (dims, ((), ())), preferred_element_type=f32)  17.3 us
    ppermute x9, starting transfers between devices, swap(): return lax.ppermute(a, 'tensor', [(t, t ^ j) for t in range(members)])  5.92 us
    ppermute x3, starting transfers between devices, across(): lax.ppermute(a, 'dp', [(at(z, x), at(z, 1 - x)) for z in range(lines) for...  4.16 us
  transfers between devices with their start and end apart: 42, of which 18 were waited for; matrix products, arithmetic and copies ran while one was open for 12% of the time, Pallas kernels for 0%

profile of v1, /device:TPU:0, one launch (start us, length us, event | category | flops | bytes accessed | tf_op | source)
XLA Modules:
  0.0 193.8 jit_solution(16032197990975039782)
XLA Ops:
  0.6 3.0 %collective-permute-start.6 = (bf16[1792,256]{1,0:T(8,128)(2,1)}, bf16[1792,256]{1,0:T(8,128)(2,1)S(1)}, u32[]{:S(2)}, u32[]{:S(2)}) collective-permute-start(bf16[1792,256]{1,0:T(8,128)(2,1)} %param.8), channel_id=1, source_target_pairs={{0,4},{4,0},{8,12},{12,8},{16,20},{20,16},{24,28},{28,24},{1,5},{5... | collective-permute-start | bytes 2752520 | tf_op jit(solution)/shard_map/ppermute | solution.py:57
  3.7 1.0 constant_dynamic-slice_fusion.7
  4.7 3.7 %collective-permute-start.2 = (bf16[48,512]{1,0:T(8,128)(2,1)S(1)}, bf16[48,512]{1,0:T(8,128)(2,1)S(1)}, u32[]{:S(2)}, u32[]{:S(2)}) collective-permute-start(bf16[48,512]{1,0:T(8,128)(2,1)S(1)} %pad_maximum_fusion.15), channel_id=1, source_target_pairs={{0,24},{4,28},{8,0},{12,4},{16,8},{20,12},{24,16},{28,20},{1,25},{... | collective-permute-start | bytes 147464 | tf_op jit(solution)/shard_map/ppermute | solution.py:54
  8.3 1.0 collective-permute-start
  9.3 0.7 collective-permute-done.2
  10.1 3.2 %collective-permute-done.1 = bf16[48,512]{1,0:T(8,128)(2,1)S(1)} collective-permute-done((bf16[48,512]{1,0:T(8,128)(2,1)S(1)}, bf16[48,512]{1,0:T(8,128)(2,1)S(1)}, u32[]{:S(2)}, u32[]{:S(2)}) %collective-permute-start.1) | collective-permute-done | bytes 49184 | tf_op jit(solution)/shard_map/ppermute | solution.py:54
  13.3 1.0 collective-permute-done
  14.3 0.7 fusion.90
  15.0 1.5 collective-permute-start.4
  16.5 2.4 %fusion.6 = bf16[192,1792]{1,0:T(8,128)(2,1)} fusion(bf16[192,1792]{1,0:T(8,128)(2,1)S(1)} %copy-done.2, bf16[192,1792]{1,0:T(8,128)(2,1)} %param.6), kind=kLoop, calls=%fused_computation.11 | loop fusion | flops 2752512 | bytes 2064384 | tf_op jit(solution)/shard_map/convert_element_type | solution.py:88
  18.9 2.1 %collective-permute-start.35 = (bf16[192,1792]{1,0:T(8,128)(2,1)}, bf16[192,1792]{1,0:T(8,128)(2,1)}, u32[]{:S(2)}, u32[]{:S(2)}) collective-permute-start(bf16[192,1792]{1,0:T(8,128)(2,1)} %fusion.6), channel_id=1, source_target_pairs={{0,8},{4,12},{8,16},{12,20},{16,24},{20,28},{1,9},{5,13},{9,17},{1... | collective-permute-start | bytes 2064392 | tf_op jit(solution)/shard_map/ppermute | solution.py:54
  21.0 1.3 collective-permute-start.36
  22.4 0.5 collective-permute-start.5
  22.9 1.0 constant_dynamic-update-slice_fusion.1
  24.0 0.5 collective-permute-start.21
  25.0 9.2 %collective-permute-done.35 = bf16[192,1792]{1,0:T(8,128)(2,1)} collective-permute-done((bf16[192,1792]{1,0:T(8,128)(2,1)}, bf16[192,1792]{1,0:T(8,128)(2,1)}, u32[]{:S(2)}, u32[]{:S(2)}) %collective-permute-start.35) | collective-permute-done | bytes 688160 | tf_op jit(solution)/shard_map/ppermute | solution.py:54
  34.1 0.7 collective-permute-start.39
  34.8 4.2 %collective-permute-done.36 = bf16[192,1792]{1,0:T(8,128)(2,1)} collective-permute-done((bf16[192,1792]{1,0:T(8,128)(2,1)}, bf16[192,1792]{1,0:T(8,128)(2,1)}, u32[]{:S(2)}, u32[]{:S(2)}) %collective-permute-start.36) | collective-permute-done | bytes 688160 | tf_op jit(solution)/shard_map/ppermute | solution.py:54
  39.1 1.3 collective-permute-start.37
  41.4 0.7 collective-permute-start.10
  42.6 0.7 collective-permute-start.17
  43.7 4.6 %collective-permute-start.7 = (bf16[192,896]{1,0:T(8,128)(2,1)S(1)}, bf16[192,896]{1,0:T(8,128)(2,1)S(1)}, u32[]{:S(2)}, u32[]{:S(2)}) collective-permute-start(bf16[192,896]{1,0:T(8,128)(2,1)S(1)} %convolution_convert_fusion.3), channel_id=1, source_target_pairs={{0,8},{4,12},{1,9},{5,13},{2,10},{6,14},{3,11},{7,15}} | collective-permute-start | bytes 1032200 | tf_op jit(solution)/shard_map/ppermute | solution.py:54
  48.3 0.5 fusion.12
  48.8 1.3 collective-permute-start.14
  50.6 6.1 %collective-permute-done.7 = bf16[192,896]{1,0:T(8,128)(2,1)S(1)} collective-permute-done((bf16[192,896]{1,0:T(8,128)(2,1)S(1)}, bf16[192,896]{1,0:T(8,128)(2,1)S(1)}, u32[]{:S(2)}, u32[]{:S(2)}) %collective-permute-start.7) | collective-permute-done | bytes 344096 | tf_op jit(solution)/shard_map/ppermute | solution.py:54
  56.7 0.7 collective-permute-start.11
  57.4 0.5 fusion.10
  57.9 3.1 %collective-permute-done.14 = bf16[192,896]{1,0:T(8,128)(2,1)S(1)} collective-permute-done((bf16[192,896]{1,0:T(8,128)(2,1)S(1)}, bf16[192,896]{1,0:T(8,128)(2,1)S(1)}, u32[]{:S(2)}, u32[]{:S(2)}) %collective-permute-start.14) | collective-permute-done | bytes 344096 | tf_op jit(solution)/shard_map/ppermute | solution.py:54
  61.0 4.4 %collective-permute-start.8 = (bf16[192,896]{1,0:T(8,128)(2,1)S(1)}, bf16[192,896]{1,0:T(8,128)(2,1)S(1)}, u32[]{:S(2)}, u32[]{:S(2)}) collective-permute-start(bf16[192,896]{1,0:T(8,128)(2,1)S(1)} %fusion.10), channel_id=1, source_target_pairs={{0,8},{4,12},{8,16},{12,20},{1,9},{5,13},{9,17},{13,21},{2,10},{6,... | collective-permute-start | bytes 1032200 | tf_op jit(solution)/shard_map/ppermute | solution.py:54
  65.9 0.7 collective-permute-start.18
  66.6 5.6 %collective-permute-start.15 = (bf16[192,896]{1,0:T(8,128)(2,1)S(1)}, bf16[192,896]{1,0:T(8,128)(2,1)S(1)}, u32[]{:S(2)}, u32[]{:S(2)}) collective-permute-start(bf16[192,896]{1,0:T(8,128)(2,1)S(1)} %fusion.14), channel_id=1, source_target_pairs={{0,8},{4,12},{8,16},{12,20},{1,9},{5,13},{9,17},{13,21},{2,10},{6,... | collective-permute-start | bytes 1032200 | tf_op jit(solution)/shard_map/ppermute | solution.py:54
  72.3 0.7 collective-permute-start.40
  73.0 0.5 fusion.11
  73.5 1.3 collective-permute-start.12
  75.3 7.2 %collective-permute-start.9 = (bf16[192,896]{1,0:T(8,128)(2,1)S(1)}, bf16[192,896]{1,0:T(8,128)(2,1)S(1)}, u32[]{:S(2)}, u32[]{:S(2)}) collective-permute-start(bf16[192,896]{1,0:T(8,128)(2,1)S(1)} %fusion.9), channel_id=1, source_target_pairs={{0,8},{4,12},{8,16},{12,20},{16,24},{20,28},{1,9},{5,13},{9,17},{1... | collective-permute-start | bytes 1032200 | tf_op jit(solution)/shard_map/ppermute | solution.py:54
  83.0 1.3 collective-permute-start.38
  84.8 1.3 collective-permute-start.19
  86.1 2.1 %collective-permute-done.9 = bf16[192,896]{1,0:T(8,128)(2,1)S(1)} collective-permute-done((bf16[192,896]{1,0:T(8,128)(2,1)S(1)}, bf16[192,896]{1,0:T(8,128)(2,1)S(1)}, u32[]{:S(2)}, u32[]{:S(2)}) %collective-permute-start.9) | collective-permute-done | bytes 344096 | tf_op jit(solution)/shard_map/ppermute | solution.py:54
  88.2 6.3 %collective-permute-start.16 = (bf16[192,896]{1,0:T(8,128)(2,1)S(1)}, bf16[192,896]{1,0:T(8,128)(2,1)S(1)}, u32[]{:S(2)}, u32[]{:S(2)}) collective-permute-start(bf16[192,896]{1,0:T(8,128)(2,1)S(1)} %fusion.13), channel_id=1, source_target_pairs={{0,8},{4,12},{8,16},{12,20},{16,24},{20,28},{1,9},{5,13},{9,17},{1... | collective-permute-start | bytes 1032200 | tf_op jit(solution)/shard_map/ppermute | solution.py:54
  94.6 0.7 fusion.32
  95.2 14.0 %collective-permute-done.19 = bf16[192,896]{1,0:T(8,128)(2,1)S(1)} collective-permute-done((bf16[192,896]{1,0:T(8,128)(2,1)S(1)}, bf16[192,896]{1,0:T(8,128)(2,1)S(1)}, u32[]{:S(2)}, u32[]{:S(2)}) %collective-permute-start.19) | collective-permute-done | bytes 344096 | tf_op jit(solution)/shard_map/ppermute | solution.py:54
  109.3 0.7 fusion.40
  109.9 12.6 %collective-permute-start.23 = (bf16[192,896]{1,0:T(8,128)(2,1)S(1)}, bf16[192,896]{1,0:T(8,128)(2,1)S(1)}, u32[]{:S(2)}, u32[]{:S(2)}) collective-permute-start(bf16[192,896]{1,0:T(8,128)(2,1)S(1)} %get-tuple-element.10), channel_id=1, source_target_pairs={{0,24},{4,28},{8,0},{12,4},{16,8},{20,12},{24,16},{28,20},{1,25},{... | collective-permute-start | bytes 1032200 | tf_op jit(solution)/shard_map/ppermute | solution.py:54
  123.9 3.4 %collective-permute-done.23 = bf16[192,896]{1,0:T(8,128)(2,1)S(1)} collective-permute-done((bf16[192,896]{1,0:T(8,128)(2,1)S(1)}, bf16[192,896]{1,0:T(8,128)(2,1)S(1)}, u32[]{:S(2)}, u32[]{:S(2)}) %collective-permute-start.23) | collective-permute-done | bytes 344096 | tf_op jit(solution)/shard_map/ppermute | solution.py:54
  127.4 2.1 %collective-permute-start.13 = (bf16[192,896]{1,0:T(8,128)(2,1)S(1)}, bf16[192,896]{1,0:T(8,128)(2,1)S(1)}, u32[]{:S(2)}, u32[]{:S(2)}) collective-permute-start(bf16[192,896]{1,0:T(8,128)(2,1)S(1)} %get-tuple-element.8), channel_id=1, source_target_pairs={{0,8},{4,12},{8,16},{12,20},{16,24},{20,28},{24,0},{28,4},{1,9},{5... | collective-permute-start | bytes 1032200 | tf_op jit(solution)/shard_map/ppermute | solution.py:54
  130.2 4.3 %collective-permute-done.20 = bf16[192,896]{1,0:T(8,128)(2,1)S(1)} collective-permute-done((bf16[192,896]{1,0:T(8,128)(2,1)S(1)}, bf16[192,896]{1,0:T(8,128)(2,1)S(1)}, u32[]{:S(2)}, u32[]{:S(2)}) %collective-permute-start.20) | collective-permute-done | bytes 344096 | tf_op jit(solution)/shard_map/ppermute | solution.py:54
  135.8 2.4 %collective-permute-done.13 = bf16[192,896]{1,0:T(8,128)(2,1)S(1)} collective-permute-done((bf16[192,896]{1,0:T(8,128)(2,1)S(1)}, bf16[192,896]{1,0:T(8,128)(2,1)S(1)}, u32[]{:S(2)}, u32[]{:S(2)}) %collective-permute-start.13) | collective-permute-done | bytes 344096 | tf_op jit(solution)/shard_map/ppermute | solution.py:54
  139.1 0.7 collective-permute-start.25
  139.7 1.2 collective-permute-start.24
  140.9 0.9 pad_maximum_fusion.3
  141.8 1.3 add.296
  143.1 1.3 add.294
  144.4 1.0 collective-permute-start.28
  145.4 1.3 collective-permute-done.25
  146.8 6.9 %collective-permute-done.29 = bf16[192,896]{1,0:T(8,128)(2,1)S(1)} collective-permute-done((bf16[192,896]{1,0:T(8,128)(2,1)S(1)}, bf16[192,896]{1,0:T(8,128)(2,1)S(1)}, u32[]{:S(2)}, u32[]{:S(2)}) %collective-permute-start.29) | collective-permute-done | bytes 344096 | tf_op jit(solution)/shard_map/ppermute | solution.py:54
  154.3 5.8 %collective-permute-done.28 = bf16[192,896]{1,0:T(8,128)(2,1)S(1)} collective-permute-done((bf16[192,896]{1,0:T(8,128)(2,1)S(1)}, bf16[192,896]{1,0:T(8,128)(2,1)S(1)}, u32[]{:S(2)}, u32[]{:S(2)}) %collective-permute-start.28) | collective-permute-done | bytes 344096 | tf_op jit(solution)/shard_map/ppermute | solution.py:54
  160.9 0.8 collective-permute-start.31
  161.7 1.0 collective-permute-start.30
  162.8 3.8 %collective-permute-start.27 = (bf16[48,512]{1,0:T(8,128)(2,1)S(1)}, bf16[48,512]{1,0:T(8,128)(2,1)S(1)}, u32[]{:S(2)}, u32[]{:S(2)}) collective-permute-start(bf16[48,512]{1,0:T(8,128)(2,1)S(1)} %get-tuple-element.41), channel_id=1, source_target_pairs={{0,24},{4,28},{8,0},{12,4},{16,8},{20,12},{24,16},{28,20},{1,25},{... | collective-permute-start | bytes 147464 | tf_op jit(solution)/shard_map/ppermute | solution.py:54
  166.7 2.0 %fusion.1 = bf16[256,1792]{1,0:T(8,128)(2,1)S(1)} fusion(bf16[192,1792]{1,0:T(8,128)(2,1)S(1)} %add.296, bf16[192,1792]{1,0:T(8,128)(2,1)S(1)} %add.295, bf16[192,1792]{1,0:T(8,128)(2,1)S(1)} %add.294, bf16[192,1792]{1,0:T(8,128)(2,1)} %fusion.6, bf16[768,512]{1,0:T(8,128)(2,1)S(1)} %bitcast.105), kind=kOutput, calls=%fused_computation.4 | convolution fusion | flops 716570624 | bytes 4063232 | tf_op jit(solution)/shard_map/dot_general | solution.py:15
  168.7 0.6 collective-permute-start.41
  169.3 2.4 %collective-permute-done.33 = bf16[48,512]{1,0:T(8,128)(2,1)S(1)} collective-permute-done((bf16[48,512]{1,0:T(8,128)(2,1)S(1)}, bf16[48,512]{1,0:T(8,128)(2,1)S(1)}, u32[]{:S(2)}, u32[]{:S(2)}) %collective-permute-start.33) | collective-permute-done | bytes 49184 | tf_op jit(solution)/shard_map/ppermute | solution.py:54
  171.9 18.6 %collective-permute-done.41 = bf16[256,1792]{1,0:T(8,128)(2,1)S(1)} collective-permute-done((bf16[256,1792]{1,0:T(8,128)(2,1)S(1)}, bf16[256,1792]{1,0:T(8,128)(2,1)S(1)}, u32[]{:S(2)}, u32[]{:S(2)}) %collective-permute-start.41) | collective-permute-done | bytes 917536 | tf_op jit(solution)/shard_map/ppermute | solution.py:57
  190.5 3.2 %fusion = f32[256,1792]{1,0:T(8,128)} fusion(bf16[256,1792]{1,0:T(8,128)(2,1)S(1)} %collective-permute-done.41, bf16[192,1792]{1,0:T(8,128)(2,1)S(1)} %add.296, bf16[192,1792]{1,0:T(8,128)(2,1)S(1)} %add.295, bf16[192,1792]{1,0:T(8,128)(2,1)S(1)} %add.294, bf16[192,1792]{1,0:T(8,128)(2,1)} %fusion.6, bf16[768,512]{1,0:T(8,128)(2,1)S(1)} %bitcast.106), kind=kOutput, calls=%fused_computation.2 | convolution fusion | flops 717029376 | bytes 5898240 | tf_op jit(solution)/shard_map/dot_general | solution.py:15
  (103 shorter events, 11.0 us)
Async XLA Ops:
  0.6 39.7 %collective-permute-start.6 = (bf16[1792,256]{1,0:T(8,128)(2,1)}, bf16[1792,256]{1,0:T(8,128)(2,1)S(1)}, u32[]{:S(2)}, u32[]{:S(2)}) collective-permute-start(bf16[1792,256]{1,0:T(8,128)(2,1)} %param.8), channel_id=1, source_target_pairs={{0,4},{4,0},{8,12},{12,8},{16,20},{20,16},{24,28},{28,24},{1,5},{5... | collective-permute-start | bytes 2752520 | tf_op jit(solution)/shard_map/ppermute | solution.py:57
  3.7 19.2 %copy-start.1 = (bf16[1792,256]{1,0:T(8,128)(2,1)S(1)}, bf16[1792,256]{1,0:T(8,128)(2,1)}, u32[]{:S(2)}) copy-start(bf16[1792,256]{1,0:T(8,128)(2,1)} %param.8) | copy-start | bytes 2752516
  3.7 12.8 %copy-start.2 = (bf16[192,1792]{1,0:T(8,128)(2,1)S(1)}, bf16[192,1792]{1,0:T(8,128)(2,1)}, u32[]{:S(2)}) copy-start(bf16[192,1792]{1,0:T(8,128)(2,1)} %param.7) | copy-start | bytes 2064388
  4.7 5.4 %collective-permute-start.2 = (bf16[48,512]{1,0:T(8,128)(2,1)S(1)}, bf16[48,512]{1,0:T(8,128)(2,1)S(1)}, u32[]{:S(2)}, u32[]{:S(2)}) collective-permute-start(bf16[48,512]{1,0:T(8,128)(2,1)S(1)} %pad_maximum_fusion.15), channel_id=1, source_target_pairs={{0,24},{4,28},{8,0},{12,4},{16,8},{20,12},{24,16},{28,20},{1,25},{... | collective-permute-start | bytes 147464 | tf_op jit(solution)/shard_map/ppermute | solution.py:54
  8.3 5.0 %collective-permute-start.1 = (bf16[48,512]{1,0:T(8,128)(2,1)S(1)}, bf16[48,512]{1,0:T(8,128)(2,1)S(1)}, u32[]{:S(2)}, u32[]{:S(2)}) collective-permute-start(bf16[48,512]{1,0:T(8,128)(2,1)S(1)} %pad_maximum_fusion.14), channel_id=1, source_target_pairs={{0,16},{4,20},{8,24},{12,28},{16,0},{20,4},{24,8},{28,12},{1,17},{... | collective-permute-start | bytes 147464 | tf_op jit(solution)/shard_map/ppermute | solution.py:54
  8.3 5.9 %collective-permute-start = (bf16[48,512]{1,0:T(8,128)(2,1)S(1)}, bf16[48,512]{1,0:T(8,128)(2,1)S(1)}, u32[]{:S(2)}, u32[]{:S(2)}) collective-permute-start(bf16[48,512]{1,0:T(8,128)(2,1)S(1)} %pad_maximum_fusion.13), channel_id=1, source_target_pairs={{0,8},{4,12},{8,16},{12,20},{16,24},{20,28},{24,0},{28,4},{1,9},{5... | collective-permute-start | bytes 147464 | tf_op jit(solution)/shard_map/ppermute | solution.py:54
  15.0 9.1 %copy-start = (bf16[256,1792]{1,0:T(8,128)(2,1)S(1)}, bf16[256,1792]{1,0:T(8,128)(2,1)}, u32[]{:S(2)}) copy-start(bf16[256,1792]{1,0:T(8,128)(2,1)} %param.9) | copy-start | bytes 2752516
  15.0 7.4 %collective-permute-start.4 = (bf16[4,48,512]{2,1,0:T(8,128)(2,1)}, bf16[4,48,512]{2,1,0:T(8,128)(2,1)S(1)}, u32[]{:S(2)}, u32[]{:S(2)}) collective-permute-start(bf16[4,48,512]{2,1,0:T(8,128)(2,1)} %get-tuple-element.30), channel_id=1, source_target_pairs={{0,2},{1,3},{2,0},{3,1},{4,6},{5,7},{6,4},{7,5},{8,10},{9,11},{10,... | collective-permute-start | bytes 589832 | tf_op jit(solution)/shard_map/ppermute | solution.py:63
  18.9 15.2 %collective-permute-start.35 = (bf16[192,1792]{1,0:T(8,128)(2,1)}, bf16[192,1792]{1,0:T(8,128)(2,1)}, u32[]{:S(2)}, u32[]{:S(2)}) collective-permute-start(bf16[192,1792]{1,0:T(8,128)(2,1)} %fusion.6), channel_id=1, source_target_pairs={{0,8},{4,12},{8,16},{12,20},{16,24},{20,28},{1,9},{5,13},{9,17},{1... | collective-permute-start | bytes 2064392 | tf_op jit(solution)/shard_map/ppermute | solution.py:54
  21.0 18.0 %collective-permute-start.36 = (bf16[192,1792]{1,0:T(8,128)(2,1)}, bf16[192,1792]{1,0:T(8,128)(2,1)}, u32[]{:S(2)}, u32[]{:S(2)}) collective-permute-start(bf16[192,1792]{1,0:T(8,128)(2,1)} %fusion.6), channel_id=1, source_target_pairs={{8,0},{12,4},{16,8},{20,12},{24,16},{28,20},{9,1},{13,5},{17,9},{2... | collective-permute-start | bytes 2064392 | tf_op jit(solution)/shard_map/ppermute | solution.py:54
  22.3 1.7 collective-permute-start.3
  22.4 2.2 %collective-permute-start.5 = (bf16[4,48,512]{2,1,0:T(8,128)(2,1)S(1)}, bf16[4,48,512]{2,1,0:T(8,128)(2,1)S(1)}, u32[]{:S(2)}, u32[]{:S(2)}) collective-permute-start(bf16[4,48,512]{2,1,0:T(8,128)(2,1)S(1)} %collective-permute-done.4), channel_id=1, source_target_pairs={{0,1},{1,0},{2,3},{3,2},{4,5},{5,4},{6,7},{7,6},{8,9},{9,8},{10,11... | collective-permute-start | bytes 589832 | tf_op jit(solution)/shard_map/ppermute | solution.py:63
  24.0 99.1 %collective-permute-start.21 = (bf16[256,1792]{1,0:T(8,128)(2,1)S(1)}, bf16[256,1792]{1,0:T(8,128)(2,1)S(1)}, u32[]{:S(2)}, u32[]{:S(2)}) collective-permute-start(bf16[256,1792]{1,0:T(8,128)(2,1)S(1)} %copy-done), channel_id=1, source_target_pairs={{0,4},{4,0},{8,12},{12,8},{16,20},{20,16},{24,28},{28,24},{1,5},{5... | collective-permute-start | bytes 2752520 | tf_op jit(solution)/shard_map/ppermute | solution.py:57
  24.8 15.6 %copy-start.5 = (bf16[1792,512]{1,0:T(8,128)(2,1)S(1)}, bf16[1792,512]{1,0:T(8,128)(2,1)}, u32[]{:S(2)}) copy-start(bf16[1792,512]{1,0:T(8,128)(2,1)} %constant_dynamic-update-slice_fusion.1) | copy-start | bytes 5505028
  34.1 31.7 %collective-permute-start.39 = (bf16[192,1792]{1,0:T(8,128)(2,1)}, bf16[192,1792]{1,0:T(8,128)(2,1)S(1)}, u32[]{:S(2)}, u32[]{:S(2)}) collective-permute-start(bf16[192,1792]{1,0:T(8,128)(2,1)} %collective-permute-done.35), channel_id=1, source_target_pairs={{8,16},{12,20},{16,24},{20,28},{9,17},{13,21},{17,25},{21,29},{10,... | collective-permute-start | bytes 2064392 | tf_op jit(solution)/shard_map/ppermute | solution.py:54
  39.1 27.5 %collective-permute-start.37 = (bf16[192,1792]{1,0:T(8,128)(2,1)}, bf16[192,1792]{1,0:T(8,128)(2,1)S(1)}, u32[]{:S(2)}, u32[]{:S(2)}) collective-permute-start(bf16[192,1792]{1,0:T(8,128)(2,1)} %collective-permute-done.36), channel_id=1, source_target_pairs={{8,0},{12,4},{16,8},{20,12},{9,1},{13,5},{17,9},{21,13},{10,2},{14... | collective-permute-start | bytes 2064392 | tf_op jit(solution)/shard_map/ppermute | solution.py:54
  41.4 2.3 %collective-permute-start.10 = (bf16[192,896]{1,0:T(8,128)(2,1)S(1)}, bf16[192,896]{1,0:T(8,128)(2,1)S(1)}, u32[]{:S(2)}, u32[]{:S(2)}) collective-permute-start(bf16[192,896]{1,0:T(8,128)(2,1)S(1)} %convolution_convert_fusion.2), channel_id=1, source_target_pairs={{24,16},{28,20},{25,17},{29,21},{26,18},{30,22},{27,19},{31,23}} | collective-permute-start | bytes 1032200 | tf_op jit(solution)/shard_map/ppermute | solution.py:54
  42.6 6.2 %collective-permute-start.17 = (bf16[192,896]{1,0:T(8,128)(2,1)S(1)}, bf16[192,896]{1,0:T(8,128)(2,1)S(1)}, u32[]{:S(2)}, u32[]{:S(2)}) collective-permute-start(bf16[192,896]{1,0:T(8,128)(2,1)S(1)} %convolution_convert_fusion), channel_id=1, source_target_pairs={{24,16},{28,20},{25,17},{29,21},{26,18},{30,22},{27,19},{31,23}} | collective-permute-start | bytes 1032200 | tf_op jit(solution)/shard_map/ppermute | solution.py:54
  43.7 13.0 %collective-permute-start.7 = (bf16[192,896]{1,0:T(8,128)(2,1)S(1)}, bf16[192,896]{1,0:T(8,128)(2,1)S(1)}, u32[]{:S(2)}, u32[]{:S(2)}) collective-permute-start(bf16[192,896]{1,0:T(8,128)(2,1)S(1)} %convolution_convert_fusion.3), channel_id=1, source_target_pairs={{0,8},{4,12},{1,9},{5,13},{2,10},{6,14},{3,11},{7,15}} | collective-permute-start | bytes 1032200 | tf_op jit(solution)/shard_map/ppermute | solution.py:54
  48.8 12.2 %collective-permute-start.14 = (bf16[192,896]{1,0:T(8,128)(2,1)S(1)}, bf16[192,896]{1,0:T(8,128)(2,1)S(1)}, u32[]{:S(2)}, u32[]{:S(2)}) collective-permute-start(bf16[192,896]{1,0:T(8,128)(2,1)S(1)} %convolution_convert_fusion.1), channel_id=1, source_target_pairs={{0,8},{4,12},{1,9},{5,13},{2,10},{6,14},{3,11},{7,15}} | collective-permute-start | bytes 1032200 | tf_op jit(solution)/shard_map/ppermute | solution.py:54
  56.7 15.6 %collective-permute-start.11 = (bf16[192,896]{1,0:T(8,128)(2,1)S(1)}, bf16[192,896]{1,0:T(8,128)(2,1)S(1)}, u32[]{:S(2)}, u32[]{:S(2)}) collective-permute-start(bf16[192,896]{1,0:T(8,128)(2,1)S(1)} %fusion.12), channel_id=1, source_target_pairs={{16,8},{20,12},{24,16},{28,20},{17,9},{21,13},{25,17},{29,21},{18,... | collective-permute-start | bytes 1032200 | tf_op jit(solution)/shard_map/ppermute | solution.py:54
  61.0 12.5 %collective-permute-start.8 = (bf16[192,896]{1,0:T(8,128)(2,1)S(1)}, bf16[192,896]{1,0:T(8,128)(2,1)S(1)}, u32[]{:S(2)}, u32[]{:S(2)}) collective-permute-start(bf16[192,896]{1,0:T(8,128)(2,1)S(1)} %fusion.10), channel_id=1, source_target_pairs={{0,8},{4,12},{8,16},{12,20},{1,9},{5,13},{9,17},{13,21},{2,10},{6,... | collective-permute-start | bytes 1032200 | tf_op jit(solution)/shard_map/ppermute | solution.py:54
  65.9 9.5 %collective-permute-start.18 = (bf16[192,896]{1,0:T(8,128)(2,1)S(1)}, bf16[192,896]{1,0:T(8,128)(2,1)S(1)}, u32[]{:S(2)}, u32[]{:S(2)}) collective-permute-start(bf16[192,896]{1,0:T(8,128)(2,1)S(1)} %fusion.16), channel_id=1, source_target_pairs={{16,8},{20,12},{24,16},{28,20},{17,9},{21,13},{25,17},{29,21},{18,... | collective-permute-start | bytes 1032200 | tf_op jit(solution)/shard_map/ppermute | solution.py:54
  66.6 16.4 %collective-permute-start.15 = (bf16[192,896]{1,0:T(8,128)(2,1)S(1)}, bf16[192,896]{1,0:T(8,128)(2,1)S(1)}, u32[]{:S(2)}, u32[]{:S(2)}) collective-permute-start(bf16[192,896]{1,0:T(8,128)(2,1)S(1)} %fusion.14), channel_id=1, source_target_pairs={{0,8},{4,12},{8,16},{12,20},{1,9},{5,13},{9,17},{13,21},{2,10},{6,... | collective-permute-start | bytes 1032200 | tf_op jit(solution)/shard_map/ppermute | solution.py:54
  72.3 68.6 %collective-permute-start.40 = (bf16[192,1792]{1,0:T(8,128)(2,1)S(1)}, bf16[192,1792]{1,0:T(8,128)(2,1)S(1)}, u32[]{:S(2)}, u32[]{:S(2)}) collective-permute-start(bf16[192,1792]{1,0:T(8,128)(2,1)S(1)} %collective-permute-done.39), channel_id=1, source_target_pairs={{16,24},{20,28},{17,25},{21,29},{18,26},{22,30},{19,27},{23,31}} | collective-permute-start | bytes 2064392 | tf_op jit(solution)/shard_map/ppermute | solution.py:54
  73.5 11.3 %collective-permute-start.12 = (bf16[192,896]{1,0:T(8,128)(2,1)S(1)}, bf16[192,896]{1,0:T(8,128)(2,1)S(1)}, u32[]{:S(2)}, u32[]{:S(2)}) collective-permute-start(bf16[192,896]{1,0:T(8,128)(2,1)S(1)} %fusion.11), channel_id=1, source_target_pairs={{8,0},{12,4},{16,8},{20,12},{24,16},{28,20},{9,1},{13,5},{17,9},{2... | collective-permute-start | bytes 1032200 | tf_op jit(solution)/shard_map/ppermute | solution.py:54
  75.3 19.2 %copy-start.3 = (bf16[192,1792]{1,0:T(8,128)(2,1)S(1)}, bf16[192,1792]{1,0:T(8,128)(2,1)}, u32[]{:S(2)}) copy-start(bf16[192,1792]{1,0:T(8,128)(2,1)} %param.7) | copy-start | bytes 2064388
  75.3 19.2 %copy-start.4 = (bf16[192,1792]{1,0:T(8,128)(2,1)S(1)}, bf16[192,1792]{1,0:T(8,128)(2,1)}, u32[]{:S(2)}) copy-start(bf16[192,1792]{1,0:T(8,128)(2,1)} %param.6) | copy-start | bytes 2064388
  75.3 12.9 %collective-permute-start.9 = (bf16[192,896]{1,0:T(8,128)(2,1)S(1)}, bf16[192,896]{1,0:T(8,128)(2,1)S(1)}, u32[]{:S(2)}, u32[]{:S(2)}) collective-permute-start(bf16[192,896]{1,0:T(8,128)(2,1)S(1)} %fusion.9), channel_id=1, source_target_pairs={{0,8},{4,12},{8,16},{12,20},{16,24},{20,28},{1,9},{5,13},{9,17},{1... | collective-permute-start | bytes 1032200 | tf_op jit(solution)/shard_map/ppermute | solution.py:54
  83.0 60.1 %collective-permute-start.38 = (bf16[192,1792]{1,0:T(8,128)(2,1)S(1)}, bf16[192,1792]{1,0:T(8,128)(2,1)S(1)}, u32[]{:S(2)}, u32[]{:S(2)}) collective-permute-start(bf16[192,1792]{1,0:T(8,128)(2,1)S(1)} %collective-permute-done.37), channel_id=1, source_target_pairs={{8,0},{12,4},{9,1},{13,5},{10,2},{14,6},{11,3},{15,7}} | collective-permute-start | bytes 2064392 | tf_op jit(solution)/shard_map/ppermute | solution.py:54
  84.8 24.4 %collective-permute-start.19 = (bf16[192,896]{1,0:T(8,128)(2,1)S(1)}, bf16[192,896]{1,0:T(8,128)(2,1)S(1)}, u32[]{:S(2)}, u32[]{:S(2)}) collective-permute-start(bf16[192,896]{1,0:T(8,128)(2,1)S(1)} %fusion.15), channel_id=1, source_target_pairs={{8,0},{12,4},{16,8},{20,12},{24,16},{28,20},{9,1},{13,5},{17,9},{2... | collective-permute-start | bytes 1032200 | tf_op jit(solution)/shard_map/ppermute | solution.py:54
  88.2 21.0 %collective-permute-start.16 = (bf16[192,896]{1,0:T(8,128)(2,1)S(1)}, bf16[192,896]{1,0:T(8,128)(2,1)S(1)}, u32[]{:S(2)}, u32[]{:S(2)}) collective-permute-start(bf16[192,896]{1,0:T(8,128)(2,1)S(1)} %fusion.13), channel_id=1, source_target_pairs={{0,8},{4,12},{8,16},{12,20},{16,24},{20,28},{1,9},{5,13},{9,17},{1... | collective-permute-start | bytes 1032200 | tf_op jit(solution)/shard_map/ppermute | solution.py:54
  109.2 25.6 %collective-permute-start.22 = (bf16[192,896]{1,0:T(8,128)(2,1)S(1)}, bf16[192,896]{1,0:T(8,128)(2,1)S(1)}, u32[]{:S(2)}, u32[]{:S(2)}) collective-permute-start(bf16[192,896]{1,0:T(8,128)(2,1)S(1)} %get-tuple-element.8), channel_id=1, source_target_pairs={{0,24},{4,28},{8,0},{12,4},{16,8},{20,12},{24,16},{28,20},{1,25},{... | collective-permute-start | bytes 1032200 | tf_op jit(solution)/shard_map/ppermute | solution.py:54
  109.9 17.4 %collective-permute-start.23 = (bf16[192,896]{1,0:T(8,128)(2,1)S(1)}, bf16[192,896]{1,0:T(8,128)(2,1)S(1)}, u32[]{:S(2)}, u32[]{:S(2)}) collective-permute-start(bf16[192,896]{1,0:T(8,128)(2,1)S(1)} %get-tuple-element.10), channel_id=1, source_target_pairs={{0,24},{4,28},{8,0},{12,4},{16,8},{20,12},{24,16},{28,20},{1,25},{... | collective-permute-start | bytes 1032200 | tf_op jit(solution)/shard_map/ppermute | solution.py:54
  123.2 11.3 %collective-permute-start.20 = (bf16[192,896]{1,0:T(8,128)(2,1)S(1)}, bf16[192,896]{1,0:T(8,128)(2,1)S(1)}, u32[]{:S(2)}, u32[]{:S(2)}) collective-permute-start(bf16[192,896]{1,0:T(8,128)(2,1)S(1)} %get-tuple-element.10), channel_id=1, source_target_pairs={{0,8},{4,12},{8,16},{12,20},{16,24},{20,28},{24,0},{28,4},{1,9},{5... | collective-permute-start | bytes 1032200 | tf_op jit(solution)/shard_map/ppermute | solution.py:54
  127.4 10.8 %collective-permute-start.13 = (bf16[192,896]{1,0:T(8,128)(2,1)S(1)}, bf16[192,896]{1,0:T(8,128)(2,1)S(1)}, u32[]{:S(2)}, u32[]{:S(2)}) collective-permute-start(bf16[192,896]{1,0:T(8,128)(2,1)S(1)} %get-tuple-element.8), channel_id=1, source_target_pairs={{0,8},{4,12},{8,16},{12,20},{16,24},{20,28},{24,0},{28,4},{1,9},{5... | collective-permute-start | bytes 1032200 | tf_op jit(solution)/shard_map/ppermute | solution.py:54
  139.0 6.4 %collective-permute-start.26 = (bf16[3,48,512]{2,1,0:T(8,128)(2,1)S(1)}, bf16[3,48,512]{2,1,0:T(8,128)(2,1)S(1)}, u32[]{:S(2)}, u32[]{:S(2)}) collective-permute-start(bf16[3,48,512]{2,1,0:T(8,128)(2,1)S(1)} %get-tuple-element.20), channel_id=1, source_target_pairs={{0,3},{1,2},{2,1},{3,0},{4,7},{5,6},{6,5},{7,4},{8,11},{9,10},{10,... | collective-permute-start | bytes 442376 | tf_op jit(solution)/shard_map/ppermute | solution.py:63
  139.1 7.6 %collective-permute-start.25 = (bf16[3,48,512]{2,1,0:T(8,128)(2,1)S(1)}, bf16[3,48,512]{2,1,0:T(8,128)(2,1)S(1)}, u32[]{:S(2)}, u32[]{:S(2)}) collective-permute-start(bf16[3,48,512]{2,1,0:T(8,128)(2,1)S(1)} %get-tuple-element.21), channel_id=1, source_target_pairs={{0,2},{1,3},{2,0},{3,1},{4,6},{5,7},{6,4},{7,5},{8,10},{9,11},{10,... | collective-permute-start | bytes 442376 | tf_op jit(solution)/shard_map/ppermute | solution.py:63
  139.7 6.9 %collective-permute-start.24 = (bf16[3,48,512]{2,1,0:T(8,128)(2,1)S(1)}, bf16[3,48,512]{2,1,0:T(8,128)(2,1)S(1)}, u32[]{:S(2)}, u32[]{:S(2)}) collective-permute-start(bf16[3,48,512]{2,1,0:T(8,128)(2,1)S(1)} %get-tuple-element.19), channel_id=1, source_target_pairs={{0,1},{1,0},{2,3},{3,2},{4,5},{5,4},{6,7},{7,6},{8,9},{9,8},{10,11... | collective-permute-start | bytes 442376 | tf_op jit(solution)/shard_map/ppermute | solution.py:63
  140.9 12.7 %collective-permute-start.29 = (bf16[192,896]{1,0:T(8,128)(2,1)S(1)}, bf16[192,896]{1,0:T(8,128)(2,1)S(1)}, u32[]{:S(2)}, u32[]{:S(2)}) collective-permute-start(bf16[192,896]{1,0:T(8,128)(2,1)S(1)} %collective-permute-done.20), channel_id=1, source_target_pairs={{0,8},{4,12},{8,16},{12,20},{16,24},{20,28},{24,0},{28,4},{1,9},{5... | collective-permute-start | bytes 1032200 | tf_op jit(solution)/shard_map/ppermute | solution.py:54
  144.4 15.7 %collective-permute-start.28 = (bf16[192,896]{1,0:T(8,128)(2,1)S(1)}, bf16[192,896]{1,0:T(8,128)(2,1)S(1)}, u32[]{:S(2)}, u32[]{:S(2)}) collective-permute-start(bf16[192,896]{1,0:T(8,128)(2,1)S(1)} %collective-permute-done.13), channel_id=1, source_target_pairs={{0,8},{4,12},{8,16},{12,20},{16,24},{20,28},{24,0},{28,4},{1,9},{5... | collective-permute-start | bytes 1032200 | tf_op jit(solution)/shard_map/ppermute | solution.py:54
  160.8 5.8 %collective-permute-start.32 = (bf16[1,48,512]{2,1,0:T(8,128)(2,1)S(1)}, bf16[1,48,512]{2,1,0:T(8,128)(2,1)S(1)}, u32[]{:S(2)}, u32[]{:S(2)}) collective-permute-start(bf16[1,48,512]{2,1,0:T(8,128)(2,1)S(1)} %get-tuple-element.27), channel_id=1, source_target_pairs={{0,3},{1,2},{2,1},{3,0},{4,7},{5,6},{6,5},{7,4},{8,11},{9,10},{10,... | collective-permute-start | bytes 147464 | tf_op jit(solution)/shard_map/ppermute | solution.py:63
  160.9 5.7 %collective-permute-start.31 = (bf16[1,48,512]{2,1,0:T(8,128)(2,1)S(1)}, bf16[1,48,512]{2,1,0:T(8,128)(2,1)S(1)}, u32[]{:S(2)}, u32[]{:S(2)}) collective-permute-start(bf16[1,48,512]{2,1,0:T(8,128)(2,1)S(1)} %get-tuple-element.28), channel_id=1, source_target_pairs={{0,2},{1,3},{2,0},{3,1},{4,6},{5,7},{6,4},{7,5},{8,10},{9,11},{10,... | collective-permute-start | bytes 147464 | tf_op jit(solution)/shard_map/ppermute | solution.py:63
  161.7 4.9 %collective-permute-start.30 = (bf16[1,48,512]{2,1,0:T(8,128)(2,1)S(1)}, bf16[1,48,512]{2,1,0:T(8,128)(2,1)S(1)}, u32[]{:S(2)}, u32[]{:S(2)}) collective-permute-start(bf16[1,48,512]{2,1,0:T(8,128)(2,1)S(1)} %get-tuple-element.26), channel_id=1, source_target_pairs={{0,1},{1,0},{2,3},{3,2},{4,5},{5,4},{6,7},{7,6},{8,9},{9,8},{10,11... | collective-permute-start | bytes 147464 | tf_op jit(solution)/shard_map/ppermute | solution.py:63
  162.7 6.6 %collective-permute-start.34 = (bf16[48,512]{1,0:T(8,128)(2,1)S(1)}, bf16[48,512]{1,0:T(8,128)(2,1)S(1)}, u32[]{:S(2)}, u32[]{:S(2)}) collective-permute-start(bf16[48,512]{1,0:T(8,128)(2,1)S(1)} %get-tuple-element.40), channel_id=1, source_target_pairs={{0,8},{4,12},{8,16},{12,20},{16,24},{20,28},{24,0},{28,4},{1,9},{5... | collective-permute-start | bytes 147464 | tf_op jit(solution)/shard_map/ppermute | solution.py:54
  162.8 6.6 %collective-permute-start.27 = (bf16[48,512]{1,0:T(8,128)(2,1)S(1)}, bf16[48,512]{1,0:T(8,128)(2,1)S(1)}, u32[]{:S(2)}, u32[]{:S(2)}) collective-permute-start(bf16[48,512]{1,0:T(8,128)(2,1)S(1)} %get-tuple-element.41), channel_id=1, source_target_pairs={{0,24},{4,28},{8,0},{12,4},{16,8},{20,12},{24,16},{28,20},{1,25},{... | collective-permute-start | bytes 147464 | tf_op jit(solution)/shard_map/ppermute | solution.py:54
  166.6 5.1 %collective-permute-start.33 = (bf16[48,512]{1,0:T(8,128)(2,1)S(1)}, bf16[48,512]{1,0:T(8,128)(2,1)S(1)}, u32[]{:S(2)}, u32[]{:S(2)}) collective-permute-start(bf16[48,512]{1,0:T(8,128)(2,1)S(1)} %fusion.87), channel_id=1, source_target_pairs={{0,16},{4,20},{8,24},{12,28},{16,0},{20,4},{24,8},{28,12},{1,17},{... | collective-permute-start | bytes 147464 | tf_op jit(solution)/shard_map/ppermute | solution.py:54
  168.7 21.8 %collective-permute-start.41 = (bf16[256,1792]{1,0:T(8,128)(2,1)S(1)}, bf16[256,1792]{1,0:T(8,128)(2,1)S(1)}, u32[]{:S(2)}, u32[]{:S(2)}) collective-permute-start(bf16[256,1792]{1,0:T(8,128)(2,1)S(1)} %fusion.1), channel_id=1, source_target_pairs={{0,4},{4,0},{8,12},{12,8},{16,20},{20,16},{24,28},{28,24},{1,5},{5... | collective-permute-start | bytes 2752520 | tf_op jit(solution)/shard_map/ppermute | solution.py:57
  171.9 21.8 %copy-start.6 = (bf16[48,2048]{1,0:T(8,128)(2,1)}, bf16[48,2048]{1,0:T(8,128)(2,1)S(1)}, u32[]{:S(2)}) copy-start(bf16[48,2048]{1,0:T(8,128)(2,1)S(1)} %select_dynamic-update-slice_fusion) | copy-start | bytes 589828

commit v2 on v1

--- a/solution.py
+++ b/solution.py
@@ -6,7 +6,7 @@
 
 COLUMNS = 2
 CHUNKS = 2
-LONGEST = 4
+LINE = 4
 
 f32, bf16 = jnp.float32, jnp.bfloat16
 
@@ -53,8 +53,9 @@
     def along(a, pairs):
         return lax.ppermute(a, "dp", [(at(i, x), at(j, x)) for i, j in pairs for x in range(COLUMNS)])
 
-    def across(a):
-        return lax.ppermute(a, "dp", [(at(z, x), at(z, 1 - x)) for z in range(lines) for x in range(COLUMNS)])
+    def across(a, places=None):
+        places = range(lines) if places is None else places
+        return lax.ppermute(a, "dp", [(at(z, x), at(z, 1 - x)) for z in places for x in range(COLUMNS)])
 
     def turn(a, k):
         return along(a, [(i, (i + k) % lines) for i in range(lines)])
@@ -62,15 +63,20 @@
     def swap(a, j):
         return lax.ppermute(a, "tensor", [(t, t ^ j) for t in range(members)])
 
+    mates = [(z, z ^ 1) for z in range(lines)]
+    inward, outward, middles = [(0, 1), (3, 2)], [(1, 0), (2, 3)], [(1, 2), (2, 1)]
+
     def piece(z):
-        first = (z % lines) * pair
         return jnp.concatenate(
-            [lax.dynamic_slice(out_grad, (0, first + x * share), (own_rows, share)) for x in (column, 1 - column)],
+            [lax.dynamic_slice(out_grad, (0, z * pair + x * share), (own_rows, share)) for x in (column, 1 - column)],
             axis=1,
         )
 
     other_down = across(down_weight)
-    groups = {0: jnp.stack([piece(spot)] + [turn(piece(spot + k), k) for k in range(1, lines)])}
+    pieces = [piece(spot ^ k) for k in range(lines)]
+    groups = {
+        0: jnp.stack(pieces[:1] + [along(pieces[k], [(z, z ^ k) for z in range(lines)]) for k in range(1, lines)])
+    }
     j = members // 2
     while j:
         for have, value in list(groups.items()):
@@ -80,30 +86,32 @@
     grads = jnp.stack(
         [lax.dynamic_index_in_dim(all_groups, member ^ t, 0, keepdims=False) for t in range(members)], axis=1
     ).reshape(lines, rows, pair)
-    grads_left = lax.optimization_barrier(grads)
 
+    grads_in = lax.optimization_barrier(grads)
+    weight = jnp.concatenate([down_weight, other_down], axis=1)
     other_up = across(up_weight)
 
     gate_f, up_f = gate_pre.astype(f32), up_pre.astype(f32)
     hidden = (gate_f * jax.nn.sigmoid(gate_f) * up_f).astype(bf16)
-    back, ahead = [hidden], [hidden]
-    for step in range(1, lines):
-        back.append(along(back[-1], [(i, i + 1) for i in range(step - 1, lines - 1)]))
-        ahead.append(along(ahead[-1], [(i + 1, i) for i in range(lines - step)]))
+    of_mate = along(hidden, mates)
+    of_middle = along(hidden, middles)
+    of_end = along(of_mate, middles)
+    near, far = along(of_middle, outward), along(of_end, outward)
+    line_hidden = jnp.concatenate([hidden, of_mate, of_end + near, of_middle + far])
 
-    weight = jnp.concatenate([down_weight, other_down], axis=1)
     gate_grads, up_grads = [], []
     for c in range(CHUNKS):
         w = chunk(weight, 0, c)
-        r = l = None
-        for step in range(1, lines):
-            send_r = dot(grads[step], w, ((1,), (1,)))
-            send_l = dot(grads_left[lines - step], w, ((1,), (1,)))
-            if r is not None:
-                send_r, send_l = send_r + r.astype(f32), send_l + l.astype(f32)
-            r = along(send_r.astype(bf16), [(i, i + 1) for i in range(step)])
-            l = along(send_l.astype(bf16), [(i, i - 1) for i in range(lines - step, lines)])
-        upstream = dot(grads[0], w, ((1,), (1,))) + r.astype(f32) + l.astype(f32)
+
+        def times(a):
+            return dot(a, w, ((1,), (1,)))
+
+        for_end = along(times(grads_in[3]).astype(bf16), inward).astype(f32)
+        for_middles = along(times(grads_in[1:3].reshape(2 * rows, pair)).astype(bf16), inward).astype(f32)
+        far = along((times(grads[2]) + for_end).astype(bf16), middles).astype(f32)
+        near = along((times(grads[3]) + for_middles[rows:]).astype(bf16), middles).astype(f32)
+        came = along((times(grads[1]) + far).astype(bf16), outward).astype(f32)
+        upstream = times(grads[0]) + came + near + for_middles[:rows]
         g, u = chunk(gate_pre, 1, c).astype(f32), chunk(up_pre, 1, c).astype(f32)
         s = jax.nn.sigmoid(g)
         gate_grads.append((upstream * u * s * (1.0 + g * (1.0 - s))).astype(bf16))
@@ -116,22 +124,17 @@
         gate_pre, up_pre, _ = lax.optimization_barrier((gate_pre, up_pre, held[0]))
     gate_grad = jnp.concatenate(gate_grads, axis=1)
 
-    line_hidden = jnp.concatenate([hidden] + [back[k] + ahead[lines - k] for k in range(1, lines)])
     both = grads.reshape(lines * rows, pair)
-    mine, other = (
-        dot(both[:, i * share : (i + 1) * share], line_hidden, ((0,), (0,))) / replicas for i in (0, 1)
-    )
+    halves = [both[:, i * share : (i + 1) * share] for i in (0, 1)]
+    other = dot(halves[1], line_hidden, ((0,), (0,))) / replicas
+    mine = lax.optimization_barrier(dot(halves[0], line_hidden, ((0,), (0,))) / replicas)
     from_pair = across(other.astype(bf16)).astype(f32)
     down_grad = mine + from_pair
 
+    both_up = jnp.concatenate([up_weight, other_up], axis=0)
+
     def product(k):
-        return jnp.concatenate(
-            [
-                sum(dot(up_grads[c][k], chunk(w, 1, c), ((1,), (1,))) for c in range(CHUNKS)).astype(bf16)
-                for w in (up_weight, other_up)
-            ],
-            axis=1,
-        )
+        return sum(dot(up_grads[c][k], chunk(both_up, 1, c), ((1,), (1,))) for c in range(CHUNKS)).astype(bf16)
 
     done = {}
     for step in range(1, lines // 2 + 1):
@@ -147,10 +150,11 @@
         total = total.astype(bf16)
         for i, k in enumerate(ks):
             done[k] = turn(total[i], lines - k) if k else total[i]
-    done = jnp.stack([done[k] for k in range(lines)])
     parts = []
     for z in range(lines):
-        block = lax.dynamic_index_in_dim(done, (z - spot) % lines, 0, keepdims=False)
+        block, ahead = done[0], (z - spot) % lines
+        for k in range(1, lines):
+            block = jnp.where(ahead == k, done[k], block)
         first, second = block[:, :share], block[:, share:]
         parts += [jnp.where(column == 0, first, second), jnp.where(column == 0, second, first)]
     return jnp.concatenate(parts, axis=1), gate_grad, down_grad
@@ -164,7 +168,7 @@
         P("tensor", "dp"),
         P("dp", "tensor"),
     )
-    short = mesh.shape["dp"] <= LONGEST * COLUMNS
+    short = mesh.shape["dp"] == LINE * COLUMNS
 
     def body(*args):
         return (shards if short else gathered)(*args)

time: 194 us -> 196 us (1.010)
  waiting for transfers between devices: 88.9 us -> 118 us
  starting transfers between devices: 76.6 us -> 49.2 us
  matrix products: 17.3 us -> 14.7 us
    ppermute x30 -> x27, starting transfers between devices: 66.5 us -> 40 us  [along(): lax.ppermute(a, 'dp', [(at(i, x), at(j, x)) for i, j in pairs for x in ra...]
    ppermute x30 -> x27, waiting for transfers between devices: 68.9 us -> 82.1 us  [along(): lax.ppermute(a, 'dp', [(at(i, x), at(j, x)) for i, j in pairs for x in ra...]
    ppermute x3, waiting for transfers between devices: 18.6 us -> 29.5 us  [across(): lax.ppermute(a, 'dp', [(at(z, x), at(z, 1 - x)) for z in places for x in...]
    ppermute x9, waiting for transfers between devices: 1.43 us -> 6.61 us  [swap(): return lax.ppermute(a, 'tensor', [(t, t ^ j) for t in range(members)])]
    dot_general x32 -> x22, matrix products: 17.3 us -> 14.7 us  [dot(): return lax.dot_general(a, b, (dims, ((), ())), preferred_element_type=f32)]
  transfers between devices with their start and end apart: 42 -> 39, of which waited for: 18 -> 16; matrix products, arithmetic and copies ran while one was open for 12% -> 11% of each run, Pallas kernels for 0% -> 0%
where the time goes in v2:
time: 196 us; the launch traced here: 195 us
  waiting for transfers between devices  118 us (60%)
  starting transfers between devices  49.2 us (25%)
  matrix products  14.7 us (8%)
  other arithmetic  7.8 us (4%)
  local copies, waits for them, and re-layouts  3.81 us (2%)
    ppermute x27, waiting for transfers between devices, along(): lax.ppermute(a, 'dp', [(at(i, x), at(j, x)) for i, j in pairs for x in ra...  82.1 us
    ppermute x27, starting transfers between devices, along(): lax.ppermute(a, 'dp', [(at(i, x), at(j, x)) for i, j in pairs for x in ra...  40 us
    ppermute x3, waiting for transfers between devices, across(): lax.ppermute(a, 'dp', [(at(z, x), at(z, 1 - x)) for z in places for x in...  29.5 us
    dot_general x22, matrix products, dot(): return lax.dot_general(a, b, (dims, ((), ())), preferred_element_type=f32)  14.7 us
    ppermute x9, waiting for transfers between devices, swap(): return lax.ppermute(a, 'tensor', [(t, t ^ j) for t in range(members)])  6.61 us
    ppermute x9, starting transfers between devices, swap(): return lax.ppermute(a, 'tensor', [(t, t ^ j) for t in range(members)])  5.37 us
  transfers between devices with their start and end apart: 39, of which 16 were waited for; matrix products, arithmetic and copies ran while one was open for 11% of the time, Pallas kernels for 0%

profile of v2, /device:TPU:0, one launch (start us, length us, event | category | flops | bytes accessed | tf_op | source)
XLA Modules:
  0.0 195.0 jit_solution(9258962940091706448)
XLA Ops:
  0.6 2.7 %fusion.5 = bf16[192,1792]{1,0:T(8,128)(2,1)} fusion(bf16[192,1792]{1,0:T(8,128)(2,1)} %param.7, bf16[192,1792]{1,0:T(8,128)(2,1)} %param.6), kind=kLoop, calls=%fused_computation.11 | loop fusion | flops 2752512 | bytes 2064384 | tf_op jit(solution)/shard_map/convert_element_type | solution.py:95
  3.3 1.5 collective-permute-start.35
  4.8 5.1 %collective-permute-start.33 = (bf16[192,1792]{1,0:T(8,128)(2,1)}, bf16[192,1792]{1,0:T(8,128)(2,1)}, u32[]{:S(2)}, u32[]{:S(2)}) collective-permute-start(bf16[192,1792]{1,0:T(8,128)(2,1)} %fusion.5), channel_id=1, source_target_pairs={{0,8},{4,12},{8,0},{12,4},{16,24},{20,28},{24,16},{28,20},{1,9},{5... | collective-permute-start | bytes 2064392 | tf_op jit(solution)/shard_map/ppermute | solution.py:54
  10.0 1.4 collective-permute-start.2
  11.6 2.8 %collective-permute-start = (bf16[48,512]{1,0:T(8,128)(2,1)S(1)}, bf16[48,512]{1,0:T(8,128)(2,1)S(1)}, u32[]{:S(2)}, u32[]{:S(2)}) collective-permute-start(bf16[48,512]{1,0:T(8,128)(2,1)S(1)} %pad_maximum_fusion.8), channel_id=1, source_target_pairs={{0,8},{4,12},{8,0},{12,4},{16,24},{20,28},{24,16},{28,20},{1,9},{5... | collective-permute-start | bytes 147464 | tf_op jit(solution)/shard_map/ppermute | solution.py:54
  14.4 14.1 %collective-permute-done.2 = bf16[48,512]{1,0:T(8,128)(2,1)S(1)} collective-permute-done((bf16[48,512]{1,0:T(8,128)(2,1)S(1)}, bf16[48,512]{1,0:T(8,128)(2,1)S(1)}, u32[]{:S(2)}, u32[]{:S(2)}) %collective-permute-start.2) | collective-permute-done | bytes 49184 | tf_op jit(solution)/shard_map/ppermute | solution.py:54
  28.6 1.5 collective-permute-start.6
  30.1 0.7 fusion.71
  30.8 1.5 collective-permute-start.4
  32.3 1.0 constant_dynamic-update-slice_fusion.1
  33.3 3.4 %collective-permute-done.4 = bf16[4,48,512]{2,1,0:T(8,128)(2,1)S(1)} collective-permute-done((bf16[4,48,512]{2,1,0:T(8,128)(2,1)}, bf16[4,48,512]{2,1,0:T(8,128)(2,1)S(1)}, u32[]{:S(2)}, u32[]{:S(2)}) %collective-permute-start.4) | collective-permute-done | bytes 196640 | tf_op jit(solution)/shard_map/ppermute | solution.py:64
  36.7 1.2 constant_dynamic-update-slice_fusion.3
  38.0 0.8 collective-permute-start.13
  39.2 0.8 collective-permute-start.34
  40.1 1.3 collective-permute-start.36
  41.4 10.5 %collective-permute-done.6 = bf16[1792,256]{1,0:T(8,128)(2,1)} collective-permute-done((bf16[1792,256]{1,0:T(8,128)(2,1)S(1)}, bf16[1792,256]{1,0:T(8,128)(2,1)}, u32[]{:S(2)}, u32[]{:S(2)}) %collective-permute-start.6) | collective-permute-done | bytes 917536 | tf_op jit(solution)/shard_map/ppermute | solution.py:58
  51.9 1.2 constant_dynamic-update-slice_fusion
  53.1 0.6 convolution_convert_fusion.1
  54.2 1.6 collective-permute-start.7
  55.9 0.5 convolution_convert_fusion.2
  56.3 1.3 collective-permute-start.10
  57.7 0.6 convolution_convert_fusion
  58.3 6.0 %collective-permute-done.7 = bf16[192,896]{1,0:T(8,128)(2,1)S(1)} collective-permute-done((bf16[192,896]{1,0:T(8,128)(2,1)S(1)}, bf16[192,896]{1,0:T(8,128)(2,1)S(1)}, u32[]{:S(2)}, u32[]{:S(2)}) %collective-permute-start.7) | collective-permute-done | bytes 344096 | tf_op jit(solution)/shard_map/ppermute | solution.py:54
  64.3 4.4 %collective-permute-start.14 = (bf16[192,896]{1,0:T(8,128)(2,1)S(1)}, bf16[192,896]{1,0:T(8,128)(2,1)S(1)}, u32[]{:S(2)}, u32[]{:S(2)}) collective-permute-start(bf16[192,896]{1,0:T(8,128)(2,1)S(1)} %convolution_convert_fusion.2), channel_id=1, source_target_pairs={{0,8},{4,12},{24,16},{28,20},{1,9},{5,13},{25,17},{29,21},{2,10},{... | collective-permute-start | bytes 1032200 | tf_op jit(solution)/shard_map/ppermute | solution.py:54
  68.7 0.5 fusion.11
  69.2 0.7 collective-permute-start.8
  69.9 11.9 %collective-permute-done.14 = bf16[192,896]{1,0:T(8,128)(2,1)S(1)} collective-permute-done((bf16[192,896]{1,0:T(8,128)(2,1)S(1)}, bf16[192,896]{1,0:T(8,128)(2,1)S(1)}, u32[]{:S(2)}, u32[]{:S(2)}) %collective-permute-start.14) | collective-permute-done | bytes 344096 | tf_op jit(solution)/shard_map/ppermute | solution.py:54
  81.8 4.4 %collective-permute-start.17 = (bf16[384,896]{1,0:T(8,128)(2,1)S(1)}, bf16[384,896]{1,0:T(8,128)(2,1)S(1)}, u32[]{:S(2)}, u32[]{:S(2)}) collective-permute-start(bf16[384,896]{1,0:T(8,128)(2,1)S(1)} %convolution_convert_fusion), channel_id=1, source_target_pairs={{0,8},{4,12},{24,16},{28,20},{1,9},{5,13},{25,17},{29,21},{2,10},{... | collective-permute-start | bytes 2064392 | tf_op jit(solution)/shard_map/ppermute | solution.py:54
  86.2 0.5 fusion.14
  86.7 0.7 collective-permute-start.15
  87.4 1.3 collective-permute-start.37
  89.4 1.3 collective-permute-start.9
  90.8 0.5 fusion.12
  91.3 0.7 collective-permute-start.11
  92.5 1.4 collective-permute-start.16
  93.9 0.7 collective-permute-done.17
  94.7 0.5 fusion.15
  95.2 0.7 collective-permute-start.18
  95.9 25.7 %collective-permute-done.9 = bf16[192,896]{1,0:T(8,128)(2,1)S(1)} collective-permute-done((bf16[192,896]{1,0:T(8,128)(2,1)S(1)}, bf16[192,896]{1,0:T(8,128)(2,1)S(1)}, u32[]{:S(2)}, u32[]{:S(2)}) %collective-permute-start.9) | collective-permute-done | bytes 344096 | tf_op jit(solution)/shard_map/ppermute | solution.py:54
  121.6 0.7 fusion.27
  122.4 2.9 %collective-permute-done.16 = bf16[192,896]{1,0:T(8,128)(2,1)S(1)} collective-permute-done((bf16[192,896]{1,0:T(8,128)(2,1)S(1)}, bf16[192,896]{1,0:T(8,128)(2,1)S(1)}, u32[]{:S(2)}, u32[]{:S(2)}) %collective-permute-start.16) | collective-permute-done | bytes 344096 | tf_op jit(solution)/shard_map/ppermute | solution.py:54
  125.3 0.7 fusion.35
  126.0 2.3 %collective-permute-start.21 = (bf16[192,896]{1,0:T(8,128)(2,1)S(1)}, bf16[192,896]{1,0:T(8,128)(2,1)S(1)}, u32[]{:S(2)}, u32[]{:S(2)}) collective-permute-start(bf16[192,896]{1,0:T(8,128)(2,1)S(1)} %get-tuple-element.10), channel_id=1, source_target_pairs={{0,24},{4,28},{8,0},{12,4},{16,8},{20,12},{24,16},{28,20},{1,25},{... | collective-permute-start | bytes 1032200 | tf_op jit(solution)/shard_map/ppermute | solution.py:54
  128.8 0.5 fusion.18
  129.3 0.9 pad_maximum_fusion.3
  130.2 1.3 add.231
  131.4 1.9 collective-permute-done.21
  133.8 3.6 %collective-permute-done.19 = bf16[192,896]{1,0:T(8,128)(2,1)S(1)} collective-permute-done((bf16[192,896]{1,0:T(8,128)(2,1)S(1)}, bf16[192,896]{1,0:T(8,128)(2,1)S(1)}, u32[]{:S(2)}, u32[]{:S(2)}) %collective-permute-start.19) | collective-permute-done | bytes 344096 | tf_op jit(solution)/shard_map/ppermute | solution.py:54
  138.3 2.7 %collective-permute-done.12 = bf16[192,896]{1,0:T(8,128)(2,1)S(1)} collective-permute-done((bf16[192,896]{1,0:T(8,128)(2,1)S(1)}, bf16[192,896]{1,0:T(8,128)(2,1)S(1)}, u32[]{:S(2)}, u32[]{:S(2)}) %collective-permute-start.12) | collective-permute-done | bytes 344096 | tf_op jit(solution)/shard_map/ppermute | solution.py:54
  141.1 0.5 fusion.16
  141.7 1.6 collective-permute-start.23
  143.6 1.9 collective-permute-start.27
  145.5 2.2 %fusion = bf16[256,1792]{1,0:T(8,128)(2,1)S(1)} fusion(bf16[192,1792]{1,0:T(8,128)(2,1)S(1)} %add.231, bf16[192,1792]{1,0:T(8,128)(2,1)S(1)} %add.230, bf16[192,1792]{1,0:T(8,128)(2,1)} %collective-permute-done.33, bf16[192,1792]{1,0:T(8,128)(2,1)} %fusion.5, bf16[768,512]{1,0:T(8,128)(2,1)S(1)} %bitcast.94), kind=kOutput, calls=%fused_computation.3 | convolution fusion | flops 716570624 | bytes 4063232 | tf_op jit(solution)/shard_map/dot_general | solution.py:15
  147.8 3.2 %collective-permute-done.23 = bf16[3,48,512]{2,1,0:T(8,128)(2,1)S(1)} collective-permute-done((bf16[3,48,512]{2,1,0:T(8,128)(2,1)S(1)}, bf16[3,48,512]{2,1,0:T(8,128)(2,1)S(1)}, u32[]{:S(2)}, u32[]{:S(2)}) %collective-permute-start.23) | collective-permute-done | bytes 147488 | tf_op jit(solution)/shard_map/ppermute | solution.py:64
  151.1 5.2 %collective-permute-done.27 = bf16[192,896]{1,0:T(8,128)(2,1)S(1)} collective-permute-done((bf16[192,896]{1,0:T(8,128)(2,1)S(1)}, bf16[192,896]{1,0:T(8,128)(2,1)S(1)}, u32[]{:S(2)}, u32[]{:S(2)}) %collective-permute-start.27) | collective-permute-done | bytes 344096 | tf_op jit(solution)/shard_map/ppermute | solution.py:54
  156.8 6.2 %collective-permute-done.26 = bf16[192,896]{1,0:T(8,128)(2,1)S(1)} collective-permute-done((bf16[192,896]{1,0:T(8,128)(2,1)S(1)}, bf16[192,896]{1,0:T(8,128)(2,1)S(1)}, u32[]{:S(2)}, u32[]{:S(2)}) %collective-permute-start.26) | collective-permute-done | bytes 344096 | tf_op jit(solution)/shard_map/ppermute | solution.py:54
  163.6 1.3 collective-permute-start.29
  164.9 0.5 collective-permute-start.28
  165.6 3.7 %collective-permute-start.32 = (bf16[48,512]{1,0:T(8,128)(2,1)S(1)}, bf16[48,512]{1,0:T(8,128)(2,1)S(1)}, u32[]{:S(2)}, u32[]{:S(2)}) collective-permute-start(bf16[48,512]{1,0:T(8,128)(2,1)S(1)} %get-tuple-element.39), channel_id=1, source_target_pairs={{0,24},{4,28},{8,0},{12,4},{16,8},{20,12},{24,16},{28,20},{1,25},{... | collective-permute-start | bytes 147464 | tf_op jit(solution)/shard_map/ppermute | solution.py:54
  169.5 2.4 %convolution_multiply_fusion.1 = f32[256,1792]{1,0:T(8,128)S(1)} fusion(bf16[192,1792]{1,0:T(8,128)(2,1)S(1)} %add.231, bf16[192,1792]{1,0:T(8,128)(2,1)S(1)} %add.230, bf16[192,1792]{1,0:T(8,128)(2,1)} %collective-permute-done.33, bf16[192,1792]{1,0:T(8,128)(2,1)} %fusion.5, bf16[768,512]{1,0:T(8,128)(2,1)S(1)} %bitcast.95), kind=kOutput, calls=%fused_computation.1 | convolution fusion | flops 716111872 | bytes 4980736 | tf_op jit(solution)/shard_map/dot_general | solution.py:15
  171.8 1.5 collective-permute-start.38
  173.3 1.1 collective-permute-done.31
  174.6 19.0 %collective-permute-done.38 = bf16[256,1792]{1,0:T(8,128)(2,1)S(1)} collective-permute-done((bf16[256,1792]{1,0:T(8,128)(2,1)S(1)}, bf16[256,1792]{1,0:T(8,128)(2,1)S(1)}, u32[]{:S(2)}, u32[]{:S(2)}) %collective-permute-start.38) | collective-permute-done | bytes 917536 | tf_op jit(solution)/shard_map/ppermute | solution.py:58
  193.6 1.4 convert_add_fusion
  (85 shorter events, 6.4 us)
Async XLA Ops:
  0.6 9.3 %copy-start.4 = (bf16[48,2048]{1,0:T(8,128)(2,1)S(1)}, bf16[48,2048]{1,0:T(8,128)(2,1)}, u32[]{:S(2)}) copy-start(bf16[48,2048]{1,0:T(8,128)(2,1)} %param.5) | copy-start | bytes 589828
  0.6 27.9 %copy-start.1 = (bf16[1792,256]{1,0:T(8,128)(2,1)S(1)}, bf16[1792,256]{1,0:T(8,128)(2,1)}, u32[]{:S(2)}) copy-start(bf16[1792,256]{1,0:T(8,128)(2,1)} %param.8) | copy-start | bytes 2752516
  3.3 36.8 %collective-permute-start.35 = (bf16[192,1792]{1,0:T(8,128)(2,1)}, bf16[192,1792]{1,0:T(8,128)(2,1)}, u32[]{:S(2)}, u32[]{:S(2)}) collective-permute-start(bf16[192,1792]{1,0:T(8,128)(2,1)} %fusion.5), channel_id=1, source_target_pairs={{8,16},{12,20},{16,8},{20,12},{9,17},{13,21},{17,9},{21,13},{10,18... | collective-permute-start | bytes 2064392 | tf_op jit(solution)/shard_map/ppermute | solution.py:54
  4.8 34.4 %collective-permute-start.33 = (bf16[192,1792]{1,0:T(8,128)(2,1)}, bf16[192,1792]{1,0:T(8,128)(2,1)}, u32[]{:S(2)}, u32[]{:S(2)}) collective-permute-start(bf16[192,1792]{1,0:T(8,128)(2,1)} %fusion.5), channel_id=1, source_target_pairs={{0,8},{4,12},{8,0},{12,4},{16,24},{20,28},{24,16},{28,20},{1,9},{5... | collective-permute-start | bytes 2064392 | tf_op jit(solution)/shard_map/ppermute | solution.py:54
  10.0 18.6 %collective-permute-start.2 = (bf16[48,512]{1,0:T(8,128)(2,1)S(1)}, bf16[48,512]{1,0:T(8,128)(2,1)S(1)}, u32[]{:S(2)}, u32[]{:S(2)}) collective-permute-start(bf16[48,512]{1,0:T(8,128)(2,1)S(1)} %pad_maximum_fusion.10), channel_id=1, source_target_pairs={{0,24},{4,28},{8,16},{12,20},{16,8},{20,12},{24,0},{28,4},{1,25},{... | collective-permute-start | bytes 147464 | tf_op jit(solution)/shard_map/ppermute | solution.py:54
  11.4 18.7 %collective-permute-start.1 = (bf16[48,512]{1,0:T(8,128)(2,1)S(1)}, bf16[48,512]{1,0:T(8,128)(2,1)S(1)}, u32[]{:S(2)}, u32[]{:S(2)}) collective-permute-start(bf16[48,512]{1,0:T(8,128)(2,1)S(1)} %pad_maximum_fusion.9), channel_id=1, source_target_pairs={{0,16},{4,20},{8,24},{12,28},{16,0},{20,4},{24,8},{28,12},{1,17},{... | collective-permute-start | bytes 147464 | tf_op jit(solution)/shard_map/ppermute | solution.py:54
  11.6 18.4 %collective-permute-start = (bf16[48,512]{1,0:T(8,128)(2,1)S(1)}, bf16[48,512]{1,0:T(8,128)(2,1)S(1)}, u32[]{:S(2)}, u32[]{:S(2)}) collective-permute-start(bf16[48,512]{1,0:T(8,128)(2,1)S(1)} %pad_maximum_fusion.8), channel_id=1, source_target_pairs={{0,8},{4,12},{8,0},{12,4},{16,24},{20,28},{24,16},{28,20},{1,9},{5... | collective-permute-start | bytes 147464 | tf_op jit(solution)/shard_map/ppermute | solution.py:54
  28.6 23.3 %collective-permute-start.6 = (bf16[1792,256]{1,0:T(8,128)(2,1)S(1)}, bf16[1792,256]{1,0:T(8,128)(2,1)}, u32[]{:S(2)}, u32[]{:S(2)}) collective-permute-start(bf16[1792,256]{1,0:T(8,128)(2,1)S(1)} %copy-done.1), channel_id=1, source_target_pairs={{0,4},{4,0},{8,12},{12,8},{16,20},{20,16},{24,28},{28,24},{1,5},{5... | collective-permute-start | bytes 2752520 | tf_op jit(solution)/shard_map/ppermute | solution.py:58
  30.8 5.9 %collective-permute-start.4 = (bf16[4,48,512]{2,1,0:T(8,128)(2,1)}, bf16[4,48,512]{2,1,0:T(8,128)(2,1)S(1)}, u32[]{:S(2)}, u32[]{:S(2)}) collective-permute-start(bf16[4,48,512]{2,1,0:T(8,128)(2,1)} %get-tuple-element.30), channel_id=1, source_target_pairs={{0,2},{1,3},{2,0},{3,1},{4,6},{5,7},{6,4},{7,5},{8,10},{9,11},{10,... | collective-permute-start | bytes 589832 | tf_op jit(solution)/shard_map/ppermute | solution.py:64
  33.3 4.7 %collective-permute-start.3 = (bf16[4,48,512]{2,1,0:T(8,128)(2,1)}, bf16[4,48,512]{2,1,0:T(8,128)(2,1)S(1)}, u32[]{:S(2)}, u32[]{:S(2)}) collective-permute-start(bf16[4,48,512]{2,1,0:T(8,128)(2,1)} %get-tuple-element.30), channel_id=1, source_target_pairs={{0,1},{1,0},{2,3},{3,2},{4,5},{5,4},{6,7},{7,6},{8,9},{9,8},{10,11... | collective-permute-start | bytes 589832 | tf_op jit(solution)/shard_map/ppermute | solution.py:64
  36.7 2.2 %collective-permute-start.5 = (bf16[4,48,512]{2,1,0:T(8,128)(2,1)S(1)}, bf16[4,48,512]{2,1,0:T(8,128)(2,1)S(1)}, u32[]{:S(2)}, u32[]{:S(2)}) collective-permute-start(bf16[4,48,512]{2,1,0:T(8,128)(2,1)S(1)} %collective-permute-done.4), channel_id=1, source_target_pairs={{0,1},{1,0},{2,3},{3,2},{4,5},{5,4},{6,7},{7,6},{8,9},{9,8},{10,11... | collective-permute-start | bytes 589832 | tf_op jit(solution)/shard_map/ppermute | solution.py:64
  38.0 31.1 %collective-permute-start.13 = (bf16[256,1792]{1,0:T(8,128)(2,1)}, bf16[256,1792]{1,0:T(8,128)(2,1)S(1)}, u32[]{:S(2)}, u32[]{:S(2)}) collective-permute-start(bf16[256,1792]{1,0:T(8,128)(2,1)} %param.9), channel_id=1, source_target_pairs={{0,4},{4,0},{8,12},{12,8},{16,20},{20,16},{24,28},{28,24},{1,5},{5... | collective-permute-start | bytes 2752520 | tf_op jit(solution)/shard_map/ppermute | solution.py:58
  39.0 12.9 %copy-start = (bf16[1792,512]{1,0:T(8,128)(2,1)S(1)}, bf16[1792,512]{1,0:T(8,128)(2,1)}, u32[]{:S(2)}) copy-start(bf16[1792,512]{1,0:T(8,128)(2,1)} %constant_dynamic-update-slice_fusion.1) | copy-start | bytes 5505028
  39.2 47.5 %collective-permute-start.34 = (bf16[192,1792]{1,0:T(8,128)(2,1)}, bf16[192,1792]{1,0:T(8,128)(2,1)S(1)}, u32[]{:S(2)}, u32[]{:S(2)}) collective-permute-start(bf16[192,1792]{1,0:T(8,128)(2,1)} %collective-permute-done.33), channel_id=1, source_target_pairs={{8,16},{12,20},{16,8},{20,12},{9,17},{13,21},{17,9},{21,13},{10,18... | collective-permute-start | bytes 2064392 | tf_op jit(solution)/shard_map/ppermute | solution.py:54
  40.1 47.3 %collective-permute-start.36 = (bf16[192,1792]{1,0:T(8,128)(2,1)}, bf16[192,1792]{1,0:T(8,128)(2,1)S(1)}, u32[]{:S(2)}, u32[]{:S(2)}) collective-permute-start(bf16[192,1792]{1,0:T(8,128)(2,1)} %collective-permute-done.35), channel_id=1, source_target_pairs={{8,0},{12,4},{16,24},{20,28},{9,1},{13,5},{17,25},{21,29},{10,2},{... | collective-permute-start | bytes 2064392 | tf_op jit(solution)/shard_map/ppermute | solution.py:54
  54.2 10.1 %collective-permute-start.7 = (bf16[192,896]{1,0:T(8,128)(2,1)S(1)}, bf16[192,896]{1,0:T(8,128)(2,1)S(1)}, u32[]{:S(2)}, u32[]{:S(2)}) collective-permute-start(bf16[192,896]{1,0:T(8,128)(2,1)S(1)} %convolution_convert_fusion.3), channel_id=1, source_target_pairs={{0,8},{4,12},{24,16},{28,20},{1,9},{5,13},{25,17},{29,21},{2,10},{... | collective-permute-start | bytes 1032200 | tf_op jit(solution)/shard_map/ppermute | solution.py:54
  56.3 34.3 %collective-permute-start.10 = (bf16[384,896]{1,0:T(8,128)(2,1)S(1)}, bf16[384,896]{1,0:T(8,128)(2,1)S(1)}, u32[]{:S(2)}, u32[]{:S(2)}) collective-permute-start(bf16[384,896]{1,0:T(8,128)(2,1)S(1)} %convolution_convert_fusion.1), channel_id=1, source_target_pairs={{0,8},{4,12},{24,16},{28,20},{1,9},{5,13},{25,17},{29,21},{2,10},{... | collective-permute-start | bytes 2064392 | tf_op jit(solution)/shard_map/ppermute | solution.py:54
  64.3 17.5 %collective-permute-start.14 = (bf16[192,896]{1,0:T(8,128)(2,1)S(1)}, bf16[192,896]{1,0:T(8,128)(2,1)S(1)}, u32[]{:S(2)}, u32[]{:S(2)}) collective-permute-start(bf16[192,896]{1,0:T(8,128)(2,1)S(1)} %convolution_convert_fusion.2), channel_id=1, source_target_pairs={{0,8},{4,12},{24,16},{28,20},{1,9},{5,13},{25,17},{29,21},{2,10},{... | collective-permute-start | bytes 1032200 | tf_op jit(solution)/shard_map/ppermute | solution.py:54
  69.2 19.7 %collective-permute-start.8 = (bf16[192,896]{1,0:T(8,128)(2,1)S(1)}, bf16[192,896]{1,0:T(8,128)(2,1)S(1)}, u32[]{:S(2)}, u32[]{:S(2)}) collective-permute-start(bf16[192,896]{1,0:T(8,128)(2,1)S(1)} %fusion.11), channel_id=1, source_target_pairs={{8,16},{12,20},{16,8},{20,12},{9,17},{13,21},{17,9},{21,13},{10,18... | collective-permute-start | bytes 1032200 | tf_op jit(solution)/shard_map/ppermute | solution.py:54
  81.8 12.8 %collective-permute-start.17 = (bf16[384,896]{1,0:T(8,128)(2,1)S(1)}, bf16[384,896]{1,0:T(8,128)(2,1)S(1)}, u32[]{:S(2)}, u32[]{:S(2)}) collective-permute-start(bf16[384,896]{1,0:T(8,128)(2,1)S(1)} %convolution_convert_fusion), channel_id=1, source_target_pairs={{0,8},{4,12},{24,16},{28,20},{1,9},{5,13},{25,17},{29,21},{2,10},{... | collective-permute-start | bytes 2064392 | tf_op jit(solution)/shard_map/ppermute | solution.py:54
  86.7 5.2 %collective-permute-start.15 = (bf16[192,896]{1,0:T(8,128)(2,1)S(1)}, bf16[192,896]{1,0:T(8,128)(2,1)S(1)}, u32[]{:S(2)}, u32[]{:S(2)}) collective-permute-start(bf16[192,896]{1,0:T(8,128)(2,1)S(1)} %fusion.14), channel_id=1, source_target_pairs={{8,16},{12,20},{16,8},{20,12},{9,17},{13,21},{17,9},{21,13},{10,18... | collective-permute-start | bytes 1032200 | tf_op jit(solution)/shard_map/ppermute | solution.py:54
  87.4 42.8 %collective-permute-start.37 = (bf16[192,1792]{1,0:T(8,128)(2,1)S(1)}, bf16[192,1792]{1,0:T(8,128)(2,1)S(1)}, u32[]{:S(2)}, u32[]{:S(2)}) collective-permute-start(bf16[192,1792]{1,0:T(8,128)(2,1)S(1)} %collective-permute-done.34), channel_id=1, source_target_pairs={{8,0},{12,4},{16,24},{20,28},{9,1},{13,5},{17,25},{21,29},{10,2},{... | collective-permute-start | bytes 2064392 | tf_op jit(solution)/shard_map/ppermute | solution.py:54
  89.4 32.2 %collective-permute-start.9 = (bf16[192,896]{1,0:T(8,128)(2,1)S(1)}, bf16[192,896]{1,0:T(8,128)(2,1)S(1)}, u32[]{:S(2)}, u32[]{:S(2)}) collective-permute-start(bf16[192,896]{1,0:T(8,128)(2,1)S(1)} %fusion.10), channel_id=1, source_target_pairs={{8,0},{12,4},{16,24},{20,28},{9,1},{13,5},{17,25},{21,29},{10,2},{... | collective-permute-start | bytes 1032200 | tf_op jit(solution)/shard_map/ppermute | solution.py:54
  91.3 30.3 %collective-permute-start.11 = (bf16[192,896]{1,0:T(8,128)(2,1)S(1)}, bf16[192,896]{1,0:T(8,128)(2,1)S(1)}, u32[]{:S(2)}, u32[]{:S(2)}) collective-permute-start(bf16[192,896]{1,0:T(8,128)(2,1)S(1)} %fusion.12), channel_id=1, source_target_pairs={{8,16},{12,20},{16,8},{20,12},{9,17},{13,21},{17,9},{21,13},{10,18... | collective-permute-start | bytes 1032200 | tf_op jit(solution)/shard_map/ppermute | solution.py:54
  92.4 29.1 %copy-start.2 = (bf16[192,1792]{1,0:T(8,128)(2,1)S(1)}, bf16[192,1792]{1,0:T(8,128)(2,1)}, u32[]{:S(2)}) copy-start(bf16[192,1792]{1,0:T(8,128)(2,1)} %param.7) | copy-start | bytes 2064388
  92.5 29.1 %copy-start.3 = (bf16[192,1792]{1,0:T(8,128)(2,1)S(1)}, bf16[192,1792]{1,0:T(8,128)(2,1)}, u32[]{:S(2)}) copy-start(bf16[192,1792]{1,0:T(8,128)(2,1)} %param.6) | copy-start | bytes 2064388
  92.5 32.8 %collective-permute-start.16 = (bf16[192,896]{1,0:T(8,128)(2,1)S(1)}, bf16[192,896]{1,0:T(8,128)(2,1)S(1)}, u32[]{:S(2)}, u32[]{:S(2)}) collective-permute-start(bf16[192,896]{1,0:T(8,128)(2,1)S(1)} %fusion.13), channel_id=1, source_target_pairs={{8,0},{12,4},{16,24},{20,28},{9,1},{13,5},{17,25},{21,29},{10,2},{... | collective-permute-start | bytes 1032200 | tf_op jit(solution)/shard_map/ppermute | solution.py:54
  95.2 30.1 %collective-permute-start.18 = (bf16[192,896]{1,0:T(8,128)(2,1)S(1)}, bf16[192,896]{1,0:T(8,128)(2,1)S(1)}, u32[]{:S(2)}, u32[]{:S(2)}) collective-permute-start(bf16[192,896]{1,0:T(8,128)(2,1)S(1)} %fusion.15), channel_id=1, source_target_pairs={{8,16},{12,20},{16,8},{20,12},{9,17},{13,21},{17,9},{21,13},{10,18... | collective-permute-start | bytes 1032200 | tf_op jit(solution)/shard_map/ppermute | solution.py:54
  122.3 15.5 %collective-permute-start.20 = (bf16[192,896]{1,0:T(8,128)(2,1)S(1)}, bf16[192,896]{1,0:T(8,128)(2,1)S(1)}, u32[]{:S(2)}, u32[]{:S(2)}) collective-permute-start(bf16[192,896]{1,0:T(8,128)(2,1)S(1)} %get-tuple-element.8), channel_id=1, source_target_pairs={{0,24},{4,28},{8,0},{12,4},{16,8},{20,12},{24,16},{28,20},{1,25},{... | collective-permute-start | bytes 1032200 | tf_op jit(solution)/shard_map/ppermute | solution.py:54
  126.0 7.3 %collective-permute-start.21 = (bf16[192,896]{1,0:T(8,128)(2,1)S(1)}, bf16[192,896]{1,0:T(8,128)(2,1)S(1)}, u32[]{:S(2)}, u32[]{:S(2)}) collective-permute-start(bf16[192,896]{1,0:T(8,128)(2,1)S(1)} %get-tuple-element.10), channel_id=1, source_target_pairs={{0,24},{4,28},{8,0},{12,4},{16,8},{20,12},{24,16},{28,20},{1,25},{... | collective-permute-start | bytes 1032200 | tf_op jit(solution)/shard_map/ppermute | solution.py:54
  128.3 9.0 %collective-permute-start.19 = (bf16[192,896]{1,0:T(8,128)(2,1)S(1)}, bf16[192,896]{1,0:T(8,128)(2,1)S(1)}, u32[]{:S(2)}, u32[]{:S(2)}) collective-permute-start(bf16[192,896]{1,0:T(8,128)(2,1)S(1)} %get-tuple-element.10), channel_id=1, source_target_pairs={{0,8},{4,12},{8,16},{12,20},{16,24},{20,28},{24,0},{28,4},{1,9},{5... | collective-permute-start | bytes 1032200 | tf_op jit(solution)/shard_map/ppermute | solution.py:54
  128.3 12.7 %collective-permute-start.12 = (bf16[192,896]{1,0:T(8,128)(2,1)S(1)}, bf16[192,896]{1,0:T(8,128)(2,1)S(1)}, u32[]{:S(2)}, u32[]{:S(2)}) collective-permute-start(bf16[192,896]{1,0:T(8,128)(2,1)S(1)} %get-tuple-element.8), channel_id=1, source_target_pairs={{0,8},{4,12},{8,16},{12,20},{16,24},{20,28},{24,0},{28,4},{1,9},{5... | collective-permute-start | bytes 1032200 | tf_op jit(solution)/shard_map/ppermute | solution.py:54
  141.7 6.2 %collective-permute-start.24 = (bf16[3,48,512]{2,1,0:T(8,128)(2,1)S(1)}, bf16[3,48,512]{2,1,0:T(8,128)(2,1)S(1)}, u32[]{:S(2)}, u32[]{:S(2)}) collective-permute-start(bf16[3,48,512]{2,1,0:T(8,128)(2,1)S(1)} %get-tuple-element.20), channel_id=1, source_target_pairs={{0,3},{1,2},{2,1},{3,0},{4,7},{5,6},{6,5},{7,4},{8,11},{9,10},{10,... | collective-permute-start | bytes 442376 | tf_op jit(solution)/shard_map/ppermute | solution.py:64
  141.7 9.3 %collective-permute-start.23 = (bf16[3,48,512]{2,1,0:T(8,128)(2,1)S(1)}, bf16[3,48,512]{2,1,0:T(8,128)(2,1)S(1)}, u32[]{:S(2)}, u32[]{:S(2)}) collective-permute-start(bf16[3,48,512]{2,1,0:T(8,128)(2,1)S(1)} %get-tuple-element.21), channel_id=1, source_target_pairs={{0,2},{1,3},{2,0},{3,1},{4,6},{5,7},{6,4},{7,5},{8,10},{9,11},{10,... | collective-permute-start | bytes 442376 | tf_op jit(solution)/shard_map/ppermute | solution.py:64
  143.4 7.7 %collective-permute-start.22 = (bf16[3,48,512]{2,1,0:T(8,128)(2,1)S(1)}, bf16[3,48,512]{2,1,0:T(8,128)(2,1)S(1)}, u32[]{:S(2)}, u32[]{:S(2)}) collective-permute-start(bf16[3,48,512]{2,1,0:T(8,128)(2,1)S(1)} %get-tuple-element.19), channel_id=1, source_target_pairs={{0,1},{1,0},{2,3},{3,2},{4,5},{5,4},{6,7},{7,6},{8,9},{9,8},{10,11... | collective-permute-start | bytes 442376 | tf_op jit(solution)/shard_map/ppermute | solution.py:64
  143.6 12.7 %collective-permute-start.27 = (bf16[192,896]{1,0:T(8,128)(2,1)S(1)}, bf16[192,896]{1,0:T(8,128)(2,1)S(1)}, u32[]{:S(2)}, u32[]{:S(2)}) collective-permute-start(bf16[192,896]{1,0:T(8,128)(2,1)S(1)} %collective-permute-done.19), channel_id=1, source_target_pairs={{0,8},{4,12},{8,16},{12,20},{16,24},{20,28},{24,0},{28,4},{1,9},{5... | collective-permute-start | bytes 1032200 | tf_op jit(solution)/shard_map/ppermute | solution.py:54
  147.7 15.3 %collective-permute-start.26 = (bf16[192,896]{1,0:T(8,128)(2,1)S(1)}, bf16[192,896]{1,0:T(8,128)(2,1)S(1)}, u32[]{:S(2)}, u32[]{:S(2)}) collective-permute-start(bf16[192,896]{1,0:T(8,128)(2,1)S(1)} %collective-permute-done.12), channel_id=1, source_target_pairs={{0,8},{4,12},{8,16},{12,20},{16,24},{20,28},{24,0},{28,4},{1,9},{5... | collective-permute-start | bytes 1032200 | tf_op jit(solution)/shard_map/ppermute | solution.py:54
  163.5 5.8 %collective-permute-start.30 = (bf16[1,48,512]{2,1,0:T(8,128)(2,1)S(1)}, bf16[1,48,512]{2,1,0:T(8,128)(2,1)S(1)}, u32[]{:S(2)}, u32[]{:S(2)}) collective-permute-start(bf16[1,48,512]{2,1,0:T(8,128)(2,1)S(1)} %get-tuple-element.27), channel_id=1, source_target_pairs={{0,3},{1,2},{2,1},{3,0},{4,7},{5,6},{6,5},{7,4},{8,11},{9,10},{10,... | collective-permute-start | bytes 147464 | tf_op jit(solution)/shard_map/ppermute | solution.py:64
  163.6 5.7 %collective-permute-start.29 = (bf16[1,48,512]{2,1,0:T(8,128)(2,1)S(1)}, bf16[1,48,512]{2,1,0:T(8,128)(2,1)S(1)}, u32[]{:S(2)}, u32[]{:S(2)}) collective-permute-start(bf16[1,48,512]{2,1,0:T(8,128)(2,1)S(1)} %get-tuple-element.28), channel_id=1, source_target_pairs={{0,2},{1,3},{2,0},{3,1},{4,6},{5,7},{6,4},{7,5},{8,10},{9,11},{10,... | collective-permute-start | bytes 147464 | tf_op jit(solution)/shard_map/ppermute | solution.py:64
  164.9 4.4 %collective-permute-start.28 = (bf16[1,48,512]{2,1,0:T(8,128)(2,1)S(1)}, bf16[1,48,512]{2,1,0:T(8,128)(2,1)S(1)}, u32[]{:S(2)}, u32[]{:S(2)}) collective-permute-start(bf16[1,48,512]{2,1,0:T(8,128)(2,1)S(1)} %get-tuple-element.26), channel_id=1, source_target_pairs={{0,1},{1,0},{2,3},{3,2},{4,5},{5,4},{6,7},{7,6},{8,9},{9,8},{10,11... | collective-permute-start | bytes 147464 | tf_op jit(solution)/shard_map/ppermute | solution.py:64
  165.5 7.8 %collective-permute-start.25 = (bf16[48,512]{1,0:T(8,128)(2,1)S(1)}, bf16[48,512]{1,0:T(8,128)(2,1)S(1)}, u32[]{:S(2)}, u32[]{:S(2)}) collective-permute-start(bf16[48,512]{1,0:T(8,128)(2,1)S(1)} %get-tuple-element.40), channel_id=1, source_target_pairs={{0,8},{4,12},{8,16},{12,20},{16,24},{20,28},{24,0},{28,4},{1,9},{5... | collective-permute-start | bytes 147464 | tf_op jit(solution)/shard_map/ppermute | solution.py:54
  165.6 7.7 %collective-permute-start.32 = (bf16[48,512]{1,0:T(8,128)(2,1)S(1)}, bf16[48,512]{1,0:T(8,128)(2,1)S(1)}, u32[]{:S(2)}, u32[]{:S(2)}) collective-permute-start(bf16[48,512]{1,0:T(8,128)(2,1)S(1)} %get-tuple-element.39), channel_id=1, source_target_pairs={{0,24},{4,28},{8,0},{12,4},{16,8},{20,12},{24,16},{28,20},{1,25},{... | collective-permute-start | bytes 147464 | tf_op jit(solution)/shard_map/ppermute | solution.py:54
  169.4 5.1 %collective-permute-start.31 = (bf16[48,512]{1,0:T(8,128)(2,1)S(1)}, bf16[48,512]{1,0:T(8,128)(2,1)S(1)}, u32[]{:S(2)}, u32[]{:S(2)}) collective-permute-start(bf16[48,512]{1,0:T(8,128)(2,1)S(1)} %fusion.68), channel_id=1, source_target_pairs={{0,16},{4,20},{8,24},{12,28},{16,0},{20,4},{24,8},{28,12},{1,17},{... | collective-permute-start | bytes 147464 | tf_op jit(solution)/shard_map/ppermute | solution.py:54
  171.8 21.8 %collective-permute-start.38 = (bf16[256,1792]{1,0:T(8,128)(2,1)S(1)}, bf16[256,1792]{1,0:T(8,128)(2,1)S(1)}, u32[]{:S(2)}, u32[]{:S(2)}) collective-permute-start(bf16[256,1792]{1,0:T(8,128)(2,1)S(1)} %fusion), channel_id=1, source_target_pairs={{0,4},{4,0},{8,12},{12,8},{16,20},{20,16},{24,28},{28,24},{1,5},{5... | collective-permute-start | bytes 2752520 | tf_op jit(solution)/shard_map/ppermute | solution.py:58
  174.6 20.4 %copy-start.5 = (bf16[48,2048]{1,0:T(8,128)(2,1)}, bf16[48,2048]{1,0:T(8,128)(2,1)S(1)}, u32[]{:S(2)}) copy-start(bf16[48,2048]{1,0:T(8,128)(2,1)S(1)} %constant_dynamic-update-slice_fusion.4) | copy-start | bytes 589828

commit v3 on v2

--- a/solution.py
+++ b/solution.py
@@ -5,6 +5,7 @@
 
 
 COLUMNS = 2
+FIRST = 5
 CHUNKS = 2
 LINE = 4
 
@@ -42,10 +43,11 @@
     rows, hidden_units = gate_pre.shape
     share = up_weight.shape[0]
     pair = COLUMNS * share
-    width = hidden_units // CHUNKS
+    first = hidden_units * FIRST // 128 // 14 * 128
+    bounds = (0, first, hidden_units)
 
     def chunk(a, axis, c):
-        return lax.slice_in_dim(a, c * width, (c + 1) * width, axis=axis)
+        return lax.slice_in_dim(a, bounds[c], bounds[c + 1], axis=axis)
 
     def at(z, x):
         return z * COLUMNS + x

time: 196 us -> 197 us (level)
  starting transfers between devices: 49.2 us -> 44.2 us
  waiting for transfers between devices: 118 us -> 123 us
    ppermute x27, waiting for transfers between devices: 82.1 us -> 87.3 us  [along(): lax.ppermute(a, 'dp', [(at(i, x), at(j, x)) for i, j in pairs for x in ra...]
    ppermute x27, starting transfers between devices: 40 us -> 35 us  [along(): lax.ppermute(a, 'dp', [(at(i, x), at(j, x)) for i, j in pairs for x in ra...]
    ppermute x3, waiting for transfers between devices: 29.5 us -> 25.5 us  [across(): lax.ppermute(a, 'dp', [(at(z, x), at(z, 1 - x)) for z in places for x in...]
    ppermute x9, waiting for transfers between devices: 6.61 us -> 10.5 us  [swap(): return lax.ppermute(a, 'tensor', [(t, t ^ j) for t in range(members)])]
  transfers between devices with their start and end apart: 39 -> 39, of which waited for: 16 -> 15; matrix products, arithmetic and copies ran while one was open for 11% -> 12% of each run, Pallas kernels for 0% -> 0%
where the time goes in v3:
time: 197 us; the launch traced here: 196 us
  waiting for transfers between devices  123 us (62%)
  starting transfers between devices  44.2 us (22%)
  matrix products  14.7 us (7%)
  other arithmetic  7.88 us (4%)
  local copies, waits for them, and re-layouts  4.49 us (2%)
    ppermute x27, waiting for transfers between devices, along(): lax.ppermute(a, 'dp', [(at(i, x), at(j, x)) for i, j in pairs for x in ra...  87.3 us
    ppermute x27, starting transfers between devices, along(): lax.ppermute(a, 'dp', [(at(i, x), at(j, x)) for i, j in pairs for x in ra...  35 us
    ppermute x3, waiting for transfers between devices, across(): lax.ppermute(a, 'dp', [(at(z, x), at(z, 1 - x)) for z in places for x in...  25.5 us
    dot_general x22, matrix products, dot(): return lax.dot_general(a, b, (dims, ((), ())), preferred_element_type=f32)  14.7 us
    ppermute x9, waiting for transfers between devices, swap(): return lax.ppermute(a, 'tensor', [(t, t ^ j) for t in range(members)])  10.5 us
    ppermute x9, starting transfers between devices, swap(): return lax.ppermute(a, 'tensor', [(t, t ^ j) for t in range(members)])  5.37 us
  transfers between devices with their start and end apart: 39, of which 15 were waited for; matrix products, arithmetic and copies ran while one was open for 12% of the time, Pallas kernels for 0%

profile of v3, /device:TPU:0, one launch (start us, length us, event | category | flops | bytes accessed | tf_op | source)
XLA Modules:
  0.0 195.9 jit_solution(18144775344409377006)
XLA Ops:
  0.6 2.7 %fusion.10 = bf16[192,1792]{1,0:T(8,128)(2,1)} fusion(bf16[192,1792]{1,0:T(8,128)(2,1)} %param.7, bf16[192,1792]{1,0:T(8,128)(2,1)} %param.6), kind=kLoop, calls=%fused_computation.22 | loop fusion | flops 2752512 | bytes 2064384 | tf_op jit(solution)/shard_map/convert_element_type | solution.py:97
  3.3 1.5 collective-permute-start.35
  4.8 5.1 %collective-permute-start.33 = (bf16[192,1792]{1,0:T(8,128)(2,1)}, bf16[192,1792]{1,0:T(8,128)(2,1)}, u32[]{:S(2)}, u32[]{:S(2)}) collective-permute-start(bf16[192,1792]{1,0:T(8,128)(2,1)} %fusion.10), channel_id=1, source_target_pairs={{0,8},{4,12},{8,0},{12,4},{16,24},{20,28},{24,16},{28,20},{1,9},{5... | collective-permute-start | bytes 2064392 | tf_op jit(solution)/shard_map/ppermute | solution.py:56
  10.0 1.4 collective-permute-start.2
  11.6 2.8 %collective-permute-start = (bf16[48,512]{1,0:T(8,128)(2,1)S(1)}, bf16[48,512]{1,0:T(8,128)(2,1)S(1)}, u32[]{:S(2)}, u32[]{:S(2)}) collective-permute-start(bf16[48,512]{1,0:T(8,128)(2,1)S(1)} %pad_maximum_fusion.8), channel_id=1, source_target_pairs={{0,8},{4,12},{8,0},{12,4},{16,24},{20,28},{24,16},{28,20},{1,9},{5... | collective-permute-start | bytes 147464 | tf_op jit(solution)/shard_map/ppermute | solution.py:56
  14.4 14.1 %collective-permute-done.2 = bf16[48,512]{1,0:T(8,128)(2,1)S(1)} collective-permute-done((bf16[48,512]{1,0:T(8,128)(2,1)S(1)}, bf16[48,512]{1,0:T(8,128)(2,1)S(1)}, u32[]{:S(2)}, u32[]{:S(2)}) %collective-permute-start.2) | collective-permute-done | bytes 49184 | tf_op jit(solution)/shard_map/ppermute | solution.py:56
  28.6 1.5 collective-permute-start.6
  30.1 0.7 fusion.71
  30.8 1.5 collective-permute-start.4
  32.3 1.0 constant_dynamic-update-slice_fusion.1
  33.3 3.4 %collective-permute-done.4 = bf16[4,48,512]{2,1,0:T(8,128)(2,1)S(1)} collective-permute-done((bf16[4,48,512]{2,1,0:T(8,128)(2,1)}, bf16[4,48,512]{2,1,0:T(8,128)(2,1)S(1)}, u32[]{:S(2)}, u32[]{:S(2)}) %collective-permute-start.4) | collective-permute-done | bytes 196640 | tf_op jit(solution)/shard_map/ppermute | solution.py:66
  36.7 1.2 constant_dynamic-update-slice_fusion.3
  38.0 0.8 collective-permute-start.13
  39.2 0.8 collective-permute-start.34
  40.1 1.3 collective-permute-start.36
  41.4 10.5 %collective-permute-done.6 = bf16[1792,256]{1,0:T(8,128)(2,1)} collective-permute-done((bf16[1792,256]{1,0:T(8,128)(2,1)S(1)}, bf16[1792,256]{1,0:T(8,128)(2,1)}, u32[]{:S(2)}, u32[]{:S(2)}) %collective-permute-start.6) | collective-permute-done | bytes 917536 | tf_op jit(solution)/shard_map/ppermute | solution.py:60
  51.9 1.2 constant_dynamic-update-slice_fusion
  53.7 1.6 collective-permute-start.10
  55.7 1.3 collective-permute-start.7
  57.0 0.6 convolution_convert_fusion.1
  57.6 0.7 convolution_convert_fusion
  58.3 9.5 %collective-permute-done.13 = bf16[256,1792]{1,0:T(8,128)(2,1)S(1)} collective-permute-done((bf16[256,1792]{1,0:T(8,128)(2,1)}, bf16[256,1792]{1,0:T(8,128)(2,1)S(1)}, u32[]{:S(2)}, u32[]{:S(2)}) %collective-permute-start.13) | collective-permute-done | bytes 917536 | tf_op jit(solution)/shard_map/ppermute | solution.py:60
  67.7 2.0 %collective-permute-start.17 = (bf16[384,1152]{1,0:T(8,128)(2,1)S(1)}, bf16[384,1152]{1,0:T(8,128)(2,1)S(1)}, u32[]{:S(2)}, u32[]{:S(2)}) collective-permute-start(bf16[384,1152]{1,0:T(8,128)(2,1)S(1)} %convolution_convert_fusion), channel_id=1, source_target_pairs={{0,8},{4,12},{24,16},{28,20},{1,9},{5,13},{25,17},{29,21},{2,10},{... | collective-permute-start | bytes 2654216 | tf_op jit(solution)/shard_map/ppermute | solution.py:56
  69.8 1.3 collective-permute-start.14
  71.5 0.7 collective-permute-start.8
  72.7 0.7 collective-permute-start.11
  73.8 21.1 %collective-permute-done.14 = bf16[192,1152]{1,0:T(8,128)(2,1)S(1)} collective-permute-done((bf16[192,1152]{1,0:T(8,128)(2,1)S(1)}, bf16[192,1152]{1,0:T(8,128)(2,1)S(1)}, u32[]{:S(2)}, u32[]{:S(2)}) %collective-permute-start.14) | collective-permute-done | bytes 442400 | tf_op jit(solution)/shard_map/ppermute | solution.py:56
  94.9 1.3 collective-permute-start.9
  96.2 0.5 fusion.4
  96.7 0.7 collective-permute-start.15
  97.5 1.3 collective-permute-start.37
  98.9 9.2 %collective-permute-done.9 = bf16[192,640]{1,0:T(8,128)(2,1)S(1)} collective-permute-done((bf16[192,640]{1,0:T(8,128)(2,1)S(1)}, bf16[192,640]{1,0:T(8,128)(2,1)S(1)}, u32[]{:S(2)}, u32[]{:S(2)}) %collective-permute-start.9) | collective-permute-done | bytes 245792 | tf_op jit(solution)/shard_map/ppermute | solution.py:56
  108.1 0.6 fusion.43
  108.7 2.6 %collective-permute-start.20 = (bf16[192,640]{1,0:T(8,128)(2,1)S(1)}, bf16[192,640]{1,0:T(8,128)(2,1)S(1)}, u32[]{:S(2)}, u32[]{:S(2)}) collective-permute-start(bf16[192,640]{1,0:T(8,128)(2,1)S(1)} %get-tuple-element.10), channel_id=1, source_target_pairs={{0,24},{4,28},{8,0},{12,4},{16,8},{20,12},{24,16},{28,20},{1,25},{... | collective-permute-start | bytes 737288 | tf_op jit(solution)/shard_map/ppermute | solution.py:56
  111.5 0.6 fusion.5
  112.0 0.7 collective-permute-start.18
  112.7 0.6 fusion.3
  113.3 1.3 collective-permute-start.16
  114.6 5.7 %collective-permute-done.12 = bf16[192,640]{1,0:T(8,128)(2,1)S(1)} collective-permute-done((bf16[192,640]{1,0:T(8,128)(2,1)S(1)}, bf16[192,640]{1,0:T(8,128)(2,1)S(1)}, u32[]{:S(2)}, u32[]{:S(2)}) %collective-permute-start.12) | collective-permute-done | bytes 245792 | tf_op jit(solution)/shard_map/ppermute | solution.py:56
  120.2 2.5 %collective-permute-start.26 = (bf16[192,640]{1,0:T(8,128)(2,1)S(1)}, bf16[192,640]{1,0:T(8,128)(2,1)S(1)}, u32[]{:S(2)}, u32[]{:S(2)}) collective-permute-start(bf16[192,640]{1,0:T(8,128)(2,1)S(1)} %collective-permute-done.12), channel_id=1, source_target_pairs={{0,8},{4,12},{8,16},{12,20},{16,24},{20,28},{24,0},{28,4},{1,9},{5... | collective-permute-start | bytes 737288 | tf_op jit(solution)/shard_map/ppermute | solution.py:56
  122.7 2.8 %collective-permute-done.37 = bf16[192,1792]{1,0:T(8,128)(2,1)S(1)} collective-permute-done((bf16[192,1792]{1,0:T(8,128)(2,1)S(1)}, bf16[192,1792]{1,0:T(8,128)(2,1)S(1)}, u32[]{:S(2)}, u32[]{:S(2)}) %collective-permute-start.37) | collective-permute-done | bytes 688160 | tf_op jit(solution)/shard_map/ppermute | solution.py:56
  125.5 1.3 add.231
  126.8 2.4 %convolution_multiply_fusion.1 = f32[256,1792]{1,0:T(8,128)S(1)} fusion(bf16[192,1792]{1,0:T(8,128)(2,1)S(1)} %add.231, bf16[192,1792]{1,0:T(8,128)(2,1)S(1)} %add.230, bf16[192,1792]{1,0:T(8,128)(2,1)} %collective-permute-done.33, bf16[192,1792]{1,0:T(8,128)(2,1)} %fusion.10, bf16[768,512]{1,0:T(8,128)(2,1)S(1)} %bitcast.94), kind=kOutput, calls=%fused_computation.2 | convolution fusion | flops 716111872 | bytes 4980736 | tf_op jit(solution)/shard_map/dot_general | solution.py:16
  129.2 2.2 %fusion.2 = bf16[256,1792]{1,0:T(8,128)(2,1)S(1)} fusion(bf16[192,1792]{1,0:T(8,128)(2,1)S(1)} %add.231, bf16[192,1792]{1,0:T(8,128)(2,1)S(1)} %add.230, bf16[192,1792]{1,0:T(8,128)(2,1)} %collective-permute-done.33, bf16[192,1792]{1,0:T(8,128)(2,1)} %fusion.10, bf16[768,512]{1,0:T(8,128)(2,1)S(1)} %bitcast.95), kind=kOutput, calls=%fused_computation.10 | convolution fusion | flops 716570624 | bytes 4063232 | tf_op jit(solution)/shard_map/dot_general | solution.py:16
  131.4 11.6 %collective-permute-done.16 = bf16[192,1152]{1,0:T(8,128)(2,1)S(1)} collective-permute-done((bf16[192,1152]{1,0:T(8,128)(2,1)S(1)}, bf16[192,1152]{1,0:T(8,128)(2,1)S(1)}, u32[]{:S(2)}, u32[]{:S(2)}) %collective-permute-start.16) | collective-permute-done | bytes 442400 | tf_op jit(solution)/shard_map/ppermute | solution.py:56
  143.0 0.9 fusion.27
  144.0 2.0 %collective-permute-start.19 = (bf16[192,1152]{1,0:T(8,128)(2,1)S(1)}, bf16[192,1152]{1,0:T(8,128)(2,1)S(1)}, u32[]{:S(2)}, u32[]{:S(2)}) collective-permute-start(bf16[192,1152]{1,0:T(8,128)(2,1)S(1)} %get-tuple-element.8), channel_id=1, source_target_pairs={{0,8},{4,12},{8,16},{12,20},{16,24},{20,28},{24,0},{28,4},{1,9},{5... | collective-permute-start | bytes 1327112 | tf_op jit(solution)/shard_map/ppermute | solution.py:56
  146.0 0.5 fusion.30
  146.9 16.2 %collective-permute-done.21 = bf16[192,1152]{1,0:T(8,128)(2,1)S(1)} collective-permute-done((bf16[192,1152]{1,0:T(8,128)(2,1)S(1)}, bf16[192,1152]{1,0:T(8,128)(2,1)S(1)}, u32[]{:S(2)}, u32[]{:S(2)}) %collective-permute-start.21) | collective-permute-done | bytes 442400 | tf_op jit(solution)/shard_map/ppermute | solution.py:56
  163.1 0.5 fusion.32
  163.6 0.5 fusion.34
  165.2 1.6 collective-permute-start.23
  167.0 0.9 pad_maximum_fusion.3
  167.9 3.3 %collective-permute-done.24 = bf16[3,48,512]{2,1,0:T(8,128)(2,1)S(1)} collective-permute-done((bf16[3,48,512]{2,1,0:T(8,128)(2,1)S(1)}, bf16[3,48,512]{2,1,0:T(8,128)(2,1)S(1)}, u32[]{:S(2)}, u32[]{:S(2)}) %collective-permute-start.24) | collective-permute-done | bytes 147488 | tf_op jit(solution)/shard_map/ppermute | solution.py:66
  171.2 1.5 collective-permute-start.38
  172.7 1.7 collective-permute-done.23
  174.6 6.6 %collective-permute-done.27 = bf16[192,1152]{1,0:T(8,128)(2,1)S(1)} collective-permute-done((bf16[192,1152]{1,0:T(8,128)(2,1)S(1)}, bf16[192,1152]{1,0:T(8,128)(2,1)S(1)}, u32[]{:S(2)}, u32[]{:S(2)}) %collective-permute-start.27) | collective-permute-done | bytes 442400 | tf_op jit(solution)/shard_map/ppermute | solution.py:56
  181.2 0.5 fusion.28
  182.2 1.3 collective-permute-start.29
  184.1 2.1 %collective-permute-done.30 = bf16[1,48,512]{2,1,0:T(8,128)(2,1)S(1)} collective-permute-done((bf16[1,48,512]{2,1,0:T(8,128)(2,1)S(1)}, bf16[1,48,512]{2,1,0:T(8,128)(2,1)S(1)}, u32[]{:S(2)}, u32[]{:S(2)}) %collective-permute-start.30) | collective-permute-done | bytes 49184 | tf_op jit(solution)/shard_map/ppermute | solution.py:66
  186.2 1.7 collective-permute-start.32
  188.1 5.5 %collective-permute-done.38 = bf16[256,1792]{1,0:T(8,128)(2,1)S(1)} collective-permute-done((bf16[256,1792]{1,0:T(8,128)(2,1)S(1)}, bf16[256,1792]{1,0:T(8,128)(2,1)S(1)}, u32[]{:S(2)}, u32[]{:S(2)}) %collective-permute-start.38) | collective-permute-done | bytes 917536 | tf_op jit(solution)/shard_map/ppermute | solution.py:60
  193.6 1.4 convert_add_fusion
  195.3 0.7 copy-done.5
  (85 shorter events, 6.2 us)
Async XLA Ops:
  0.6 9.3 %copy-start.4 = (bf16[48,2048]{1,0:T(8,128)(2,1)S(1)}, bf16[48,2048]{1,0:T(8,128)(2,1)}, u32[]{:S(2)}) copy-start(bf16[48,2048]{1,0:T(8,128)(2,1)} %param.5) | copy-start | bytes 589828
  0.6 27.9 %copy-start.1 = (bf16[1792,256]{1,0:T(8,128)(2,1)S(1)}, bf16[1792,256]{1,0:T(8,128)(2,1)}, u32[]{:S(2)}) copy-start(bf16[1792,256]{1,0:T(8,128)(2,1)} %param.8) | copy-start | bytes 2752516
  3.3 36.8 %collective-permute-start.35 = (bf16[192,1792]{1,0:T(8,128)(2,1)}, bf16[192,1792]{1,0:T(8,128)(2,1)}, u32[]{:S(2)}, u32[]{:S(2)}) collective-permute-start(bf16[192,1792]{1,0:T(8,128)(2,1)} %fusion.10), channel_id=1, source_target_pairs={{8,16},{12,20},{16,8},{20,12},{9,17},{13,21},{17,9},{21,13},{10,18... | collective-permute-start | bytes 2064392 | tf_op jit(solution)/shard_map/ppermute | solution.py:56
  4.8 34.4 %collective-permute-start.33 = (bf16[192,1792]{1,0:T(8,128)(2,1)}, bf16[192,1792]{1,0:T(8,128)(2,1)}, u32[]{:S(2)}, u32[]{:S(2)}) collective-permute-start(bf16[192,1792]{1,0:T(8,128)(2,1)} %fusion.10), channel_id=1, source_target_pairs={{0,8},{4,12},{8,0},{12,4},{16,24},{20,28},{24,16},{28,20},{1,9},{5... | collective-permute-start | bytes 2064392 | tf_op jit(solution)/shard_map/ppermute | solution.py:56
  10.0 18.6 %collective-permute-start.2 = (bf16[48,512]{1,0:T(8,128)(2,1)S(1)}, bf16[48,512]{1,0:T(8,128)(2,1)S(1)}, u32[]{:S(2)}, u32[]{:S(2)}) collective-permute-start(bf16[48,512]{1,0:T(8,128)(2,1)S(1)} %pad_maximum_fusion.10), channel_id=1, source_target_pairs={{0,24},{4,28},{8,16},{12,20},{16,8},{20,12},{24,0},{28,4},{1,25},{... | collective-permute-start | bytes 147464 | tf_op jit(solution)/shard_map/ppermute | solution.py:56
  11.4 18.7 %collective-permute-start.1 = (bf16[48,512]{1,0:T(8,128)(2,1)S(1)}, bf16[48,512]{1,0:T(8,128)(2,1)S(1)}, u32[]{:S(2)}, u32[]{:S(2)}) collective-permute-start(bf16[48,512]{1,0:T(8,128)(2,1)S(1)} %pad_maximum_fusion.9), channel_id=1, source_target_pairs={{0,16},{4,20},{8,24},{12,28},{16,0},{20,4},{24,8},{28,12},{1,17},{... | collective-permute-start | bytes 147464 | tf_op jit(solution)/shard_map/ppermute | solution.py:56
  11.6 18.4 %collective-permute-start = (bf16[48,512]{1,0:T(8,128)(2,1)S(1)}, bf16[48,512]{1,0:T(8,128)(2,1)S(1)}, u32[]{:S(2)}, u32[]{:S(2)}) collective-permute-start(bf16[48,512]{1,0:T(8,128)(2,1)S(1)} %pad_maximum_fusion.8), channel_id=1, source_target_pairs={{0,8},{4,12},{8,0},{12,4},{16,24},{20,28},{24,16},{28,20},{1,9},{5... | collective-permute-start | bytes 147464 | tf_op jit(solution)/shard_map/ppermute | solution.py:56
  28.6 23.3 %collective-permute-start.6 = (bf16[1792,256]{1,0:T(8,128)(2,1)S(1)}, bf16[1792,256]{1,0:T(8,128)(2,1)}, u32[]{:S(2)}, u32[]{:S(2)}) collective-permute-start(bf16[1792,256]{1,0:T(8,128)(2,1)S(1)} %copy-done.1), channel_id=1, source_target_pairs={{0,4},{4,0},{8,12},{12,8},{16,20},{20,16},{24,28},{28,24},{1,5},{5... | collective-permute-start | bytes 2752520 | tf_op jit(solution)/shard_map/ppermute | solution.py:60
  30.8 5.9 %collective-permute-start.4 = (bf16[4,48,512]{2,1,0:T(8,128)(2,1)}, bf16[4,48,512]{2,1,0:T(8,128)(2,1)S(1)}, u32[]{:S(2)}, u32[]{:S(2)}) collective-permute-start(bf16[4,48,512]{2,1,0:T(8,128)(2,1)} %get-tuple-element.30), channel_id=1, source_target_pairs={{0,2},{1,3},{2,0},{3,1},{4,6},{5,7},{6,4},{7,5},{8,10},{9,11},{10,... | collective-permute-start | bytes 589832 | tf_op jit(solution)/shard_map/ppermute | solution.py:66
  33.3 4.7 %collective-permute-start.3 = (bf16[4,48,512]{2,1,0:T(8,128)(2,1)}, bf16[4,48,512]{2,1,0:T(8,128)(2,1)S(1)}, u32[]{:S(2)}, u32[]{:S(2)}) collective-permute-start(bf16[4,48,512]{2,1,0:T(8,128)(2,1)} %get-tuple-element.30), channel_id=1, source_target_pairs={{0,1},{1,0},{2,3},{3,2},{4,5},{5,4},{6,7},{7,6},{8,9},{9,8},{10,11... | collective-permute-start | bytes 589832 | tf_op jit(solution)/shard_map/ppermute | solution.py:66
  36.7 2.2 %collective-permute-start.5 = (bf16[4,48,512]{2,1,0:T(8,128)(2,1)S(1)}, bf16[4,48,512]{2,1,0:T(8,128)(2,1)S(1)}, u32[]{:S(2)}, u32[]{:S(2)}) collective-permute-start(bf16[4,48,512]{2,1,0:T(8,128)(2,1)S(1)} %collective-permute-done.4), channel_id=1, source_target_pairs={{0,1},{1,0},{2,3},{3,2},{4,5},{5,4},{6,7},{7,6},{8,9},{9,8},{10,11... | collective-permute-start | bytes 589832 | tf_op jit(solution)/shard_map/ppermute | solution.py:66
  38.0 29.7 %collective-permute-start.13 = (bf16[256,1792]{1,0:T(8,128)(2,1)}, bf16[256,1792]{1,0:T(8,128)(2,1)S(1)}, u32[]{:S(2)}, u32[]{:S(2)}) collective-permute-start(bf16[256,1792]{1,0:T(8,128)(2,1)} %param.9), channel_id=1, source_target_pairs={{0,4},{4,0},{8,12},{12,8},{16,20},{20,16},{24,28},{28,24},{1,5},{5... | collective-permute-start | bytes 2752520 | tf_op jit(solution)/shard_map/ppermute | solution.py:60
  39.0 12.9 %copy-start = (bf16[1792,512]{1,0:T(8,128)(2,1)S(1)}, bf16[1792,512]{1,0:T(8,128)(2,1)}, u32[]{:S(2)}) copy-start(bf16[1792,512]{1,0:T(8,128)(2,1)} %constant_dynamic-update-slice_fusion.1) | copy-start | bytes 5505028
  39.2 57.5 %collective-permute-start.34 = (bf16[192,1792]{1,0:T(8,128)(2,1)}, bf16[192,1792]{1,0:T(8,128)(2,1)S(1)}, u32[]{:S(2)}, u32[]{:S(2)}) collective-permute-start(bf16[192,1792]{1,0:T(8,128)(2,1)} %collective-permute-done.33), channel_id=1, source_target_pairs={{8,16},{12,20},{16,8},{20,12},{9,17},{13,21},{17,9},{21,13},{10,18... | collective-permute-start | bytes 2064392 | tf_op jit(solution)/shard_map/ppermute | solution.py:56
  40.1 57.3 %collective-permute-start.36 = (bf16[192,1792]{1,0:T(8,128)(2,1)}, bf16[192,1792]{1,0:T(8,128)(2,1)S(1)}, u32[]{:S(2)}, u32[]{:S(2)}) collective-permute-start(bf16[192,1792]{1,0:T(8,128)(2,1)} %collective-permute-done.35), channel_id=1, source_target_pairs={{8,0},{12,4},{16,24},{20,28},{9,1},{13,5},{17,25},{21,29},{10,2},{... | collective-permute-start | bytes 2064392 | tf_op jit(solution)/shard_map/ppermute | solution.py:56
  53.7 17.8 %collective-permute-start.10 = (bf16[384,640]{1,0:T(8,128)(2,1)S(1)}, bf16[384,640]{1,0:T(8,128)(2,1)S(1)}, u32[]{:S(2)}, u32[]{:S(2)}) collective-permute-start(bf16[384,640]{1,0:T(8,128)(2,1)S(1)} %convolution_convert_fusion.2), channel_id=1, source_target_pairs={{0,8},{4,12},{24,16},{28,20},{1,9},{5,13},{25,17},{29,21},{2,10},{... | collective-permute-start | bytes 1474568 | tf_op jit(solution)/shard_map/ppermute | solution.py:56
  55.7 14.1 %collective-permute-start.7 = (bf16[192,640]{1,0:T(8,128)(2,1)S(1)}, bf16[192,640]{1,0:T(8,128)(2,1)S(1)}, u32[]{:S(2)}, u32[]{:S(2)}) collective-permute-start(bf16[192,640]{1,0:T(8,128)(2,1)S(1)} %convolution_convert_fusion.3), channel_id=1, source_target_pairs={{0,8},{4,12},{24,16},{28,20},{1,9},{5,13},{25,17},{29,21},{2,10},{... | collective-permute-start | bytes 737288 | tf_op jit(solution)/shard_map/ppermute | solution.py:56
  67.7 43.6 %collective-permute-start.17 = (bf16[384,1152]{1,0:T(8,128)(2,1)S(1)}, bf16[384,1152]{1,0:T(8,128)(2,1)S(1)}, u32[]{:S(2)}, u32[]{:S(2)}) collective-permute-start(bf16[384,1152]{1,0:T(8,128)(2,1)S(1)} %convolution_convert_fusion), channel_id=1, source_target_pairs={{0,8},{4,12},{24,16},{28,20},{1,9},{5,13},{25,17},{29,21},{2,10},{... | collective-permute-start | bytes 2654216 | tf_op jit(solution)/shard_map/ppermute | solution.py:56
  69.8 25.1 %collective-permute-start.14 = (bf16[192,1152]{1,0:T(8,128)(2,1)S(1)}, bf16[192,1152]{1,0:T(8,128)(2,1)S(1)}, u32[]{:S(2)}, u32[]{:S(2)}) collective-permute-start(bf16[192,1152]{1,0:T(8,128)(2,1)S(1)} %convolution_convert_fusion.1), channel_id=1, source_target_pairs={{0,8},{4,12},{24,16},{28,20},{1,9},{5,13},{25,17},{29,21},{2,10},{... | collective-permute-start | bytes 1327112 | tf_op jit(solution)/shard_map/ppermute | solution.py:56
  71.5 1.1 collective-permute-start.8
  72.7 26.3 %collective-permute-start.11 = (bf16[192,640]{1,0:T(8,128)(2,1)S(1)}, bf16[192,640]{1,0:T(8,128)(2,1)S(1)}, u32[]{:S(2)}, u32[]{:S(2)}) collective-permute-start(bf16[192,640]{1,0:T(8,128)(2,1)S(1)} %fusion.15), channel_id=1, source_target_pairs={{8,16},{12,20},{16,8},{20,12},{9,17},{13,21},{17,9},{21,13},{10,18... | collective-permute-start | bytes 737288 | tf_op jit(solution)/shard_map/ppermute | solution.py:56
  73.7 34.4 %copy-start.2 = (bf16[192,1792]{1,0:T(8,128)(2,1)S(1)}, bf16[192,1792]{1,0:T(8,128)(2,1)}, u32[]{:S(2)}) copy-start(bf16[192,1792]{1,0:T(8,128)(2,1)} %param.7) | copy-start | bytes 2064388
  73.7 34.4 %copy-start.3 = (bf16[192,1792]{1,0:T(8,128)(2,1)S(1)}, bf16[192,1792]{1,0:T(8,128)(2,1)}, u32[]{:S(2)}) copy-start(bf16[192,1792]{1,0:T(8,128)(2,1)} %param.6) | copy-start | bytes 2064388
  94.9 13.2 %collective-permute-start.9 = (bf16[192,640]{1,0:T(8,128)(2,1)S(1)}, bf16[192,640]{1,0:T(8,128)(2,1)S(1)}, u32[]{:S(2)}, u32[]{:S(2)}) collective-permute-start(bf16[192,640]{1,0:T(8,128)(2,1)S(1)} %fusion.13), channel_id=1, source_target_pairs={{8,0},{12,4},{16,24},{20,28},{9,1},{13,5},{17,25},{21,29},{10,2},{... | collective-permute-start | bytes 737288 | tf_op jit(solution)/shard_map/ppermute | solution.py:56
  96.7 16.0 %collective-permute-start.15 = (bf16[192,1152]{1,0:T(8,128)(2,1)S(1)}, bf16[192,1152]{1,0:T(8,128)(2,1)S(1)}, u32[]{:S(2)}, u32[]{:S(2)}) collective-permute-start(bf16[192,1152]{1,0:T(8,128)(2,1)S(1)} %fusion.4), channel_id=1, source_target_pairs={{8,16},{12,20},{16,8},{20,12},{9,17},{13,21},{17,9},{21,13},{10,18... | collective-permute-start | bytes 1327112 | tf_op jit(solution)/shard_map/ppermute | solution.py:56
  97.5 28.1 %collective-permute-start.37 = (bf16[192,1792]{1,0:T(8,128)(2,1)S(1)}, bf16[192,1792]{1,0:T(8,128)(2,1)S(1)}, u32[]{:S(2)}, u32[]{:S(2)}) collective-permute-start(bf16[192,1792]{1,0:T(8,128)(2,1)S(1)} %collective-permute-done.34), channel_id=1, source_target_pairs={{8,0},{12,4},{16,24},{20,28},{9,1},{13,5},{17,25},{21,29},{10,2},{... | collective-permute-start | bytes 2064392 | tf_op jit(solution)/shard_map/ppermute | solution.py:56
  108.7 55.9 %collective-permute-start.20 = (bf16[192,640]{1,0:T(8,128)(2,1)S(1)}, bf16[192,640]{1,0:T(8,128)(2,1)S(1)}, u32[]{:S(2)}, u32[]{:S(2)}) collective-permute-start(bf16[192,640]{1,0:T(8,128)(2,1)S(1)} %get-tuple-element.10), channel_id=1, source_target_pairs={{0,24},{4,28},{8,0},{12,4},{16,8},{20,12},{24,16},{28,20},{1,25},{... | collective-permute-start | bytes 737288 | tf_op jit(solution)/shard_map/ppermute | solution.py:56
  111.3 8.9 %collective-permute-start.12 = (bf16[192,640]{1,0:T(8,128)(2,1)S(1)}, bf16[192,640]{1,0:T(8,128)(2,1)S(1)}, u32[]{:S(2)}, u32[]{:S(2)}) collective-permute-start(bf16[192,640]{1,0:T(8,128)(2,1)S(1)} %get-tuple-element.10), channel_id=1, source_target_pairs={{0,8},{4,12},{8,16},{12,20},{16,24},{20,28},{24,0},{28,4},{1,9},{5... | collective-permute-start | bytes 737288 | tf_op jit(solution)/shard_map/ppermute | solution.py:56
  112.0 19.4 %collective-permute-start.18 = (bf16[192,1152]{1,0:T(8,128)(2,1)S(1)}, bf16[192,1152]{1,0:T(8,128)(2,1)S(1)}, u32[]{:S(2)}, u32[]{:S(2)}) collective-permute-start(bf16[192,1152]{1,0:T(8,128)(2,1)S(1)} %fusion.5), channel_id=1, source_target_pairs={{8,16},{12,20},{16,8},{20,12},{9,17},{13,21},{17,9},{21,13},{10,18... | collective-permute-start | bytes 1327112 | tf_op jit(solution)/shard_map/ppermute | solution.py:56
  113.3 29.7 %collective-permute-start.16 = (bf16[192,1152]{1,0:T(8,128)(2,1)S(1)}, bf16[192,1152]{1,0:T(8,128)(2,1)S(1)}, u32[]{:S(2)}, u32[]{:S(2)}) collective-permute-start(bf16[192,1152]{1,0:T(8,128)(2,1)S(1)} %fusion.3), channel_id=1, source_target_pairs={{8,0},{12,4},{16,24},{20,28},{9,1},{13,5},{17,25},{21,29},{10,2},{... | collective-permute-start | bytes 1327112 | tf_op jit(solution)/shard_map/ppermute | solution.py:56
  120.2 61.5 %collective-permute-start.26 = (bf16[192,640]{1,0:T(8,128)(2,1)S(1)}, bf16[192,640]{1,0:T(8,128)(2,1)S(1)}, u32[]{:S(2)}, u32[]{:S(2)}) collective-permute-start(bf16[192,640]{1,0:T(8,128)(2,1)S(1)} %collective-permute-done.12), channel_id=1, source_target_pairs={{0,8},{4,12},{8,16},{12,20},{16,24},{20,28},{24,0},{28,4},{1,9},{5... | collective-permute-start | bytes 737288 | tf_op jit(solution)/shard_map/ppermute | solution.py:56
  143.9 19.2 %collective-permute-start.21 = (bf16[192,1152]{1,0:T(8,128)(2,1)S(1)}, bf16[192,1152]{1,0:T(8,128)(2,1)S(1)}, u32[]{:S(2)}, u32[]{:S(2)}) collective-permute-start(bf16[192,1152]{1,0:T(8,128)(2,1)S(1)} %get-tuple-element.8), channel_id=1, source_target_pairs={{0,24},{4,28},{8,0},{12,4},{16,8},{20,12},{24,16},{28,20},{1,25},{... | collective-permute-start | bytes 1327112 | tf_op jit(solution)/shard_map/ppermute | solution.py:56
  144.0 19.7 %collective-permute-start.19 = (bf16[192,1152]{1,0:T(8,128)(2,1)S(1)}, bf16[192,1152]{1,0:T(8,128)(2,1)S(1)}, u32[]{:S(2)}, u32[]{:S(2)}) collective-permute-start(bf16[192,1152]{1,0:T(8,128)(2,1)S(1)} %get-tuple-element.8), channel_id=1, source_target_pairs={{0,8},{4,12},{8,16},{12,20},{16,24},{20,28},{24,0},{28,4},{1,9},{5... | collective-permute-start | bytes 1327112 | tf_op jit(solution)/shard_map/ppermute | solution.py:56
  165.1 6.1 %collective-permute-start.24 = (bf16[3,48,512]{2,1,0:T(8,128)(2,1)S(1)}, bf16[3,48,512]{2,1,0:T(8,128)(2,1)S(1)}, u32[]{:S(2)}, u32[]{:S(2)}) collective-permute-start(bf16[3,48,512]{2,1,0:T(8,128)(2,1)S(1)} %get-tuple-element.20), channel_id=1, source_target_pairs={{0,3},{1,2},{2,1},{3,0},{4,7},{5,6},{6,5},{7,4},{8,11},{9,10},{10,... | collective-permute-start | bytes 442376 | tf_op jit(solution)/shard_map/ppermute | solution.py:66
  165.2 9.3 %collective-permute-start.23 = (bf16[3,48,512]{2,1,0:T(8,128)(2,1)S(1)}, bf16[3,48,512]{2,1,0:T(8,128)(2,1)S(1)}, u32[]{:S(2)}, u32[]{:S(2)}) collective-permute-start(bf16[3,48,512]{2,1,0:T(8,128)(2,1)S(1)} %get-tuple-element.21), channel_id=1, source_target_pairs={{0,2},{1,3},{2,0},{3,1},{4,6},{5,7},{6,4},{7,5},{8,10},{9,11},{10,... | collective-permute-start | bytes 442376 | tf_op jit(solution)/shard_map/ppermute | solution.py:66
  166.8 7.7 %collective-permute-start.22 = (bf16[3,48,512]{2,1,0:T(8,128)(2,1)S(1)}, bf16[3,48,512]{2,1,0:T(8,128)(2,1)S(1)}, u32[]{:S(2)}, u32[]{:S(2)}) collective-permute-start(bf16[3,48,512]{2,1,0:T(8,128)(2,1)S(1)} %get-tuple-element.19), channel_id=1, source_target_pairs={{0,1},{1,0},{2,3},{3,2},{4,5},{5,4},{6,7},{7,6},{8,9},{9,8},{10,11... | collective-permute-start | bytes 442376 | tf_op jit(solution)/shard_map/ppermute | solution.py:66
  167.0 14.1 %collective-permute-start.27 = (bf16[192,1152]{1,0:T(8,128)(2,1)S(1)}, bf16[192,1152]{1,0:T(8,128)(2,1)S(1)}, u32[]{:S(2)}, u32[]{:S(2)}) collective-permute-start(bf16[192,1152]{1,0:T(8,128)(2,1)S(1)} %collective-permute-done.19), channel_id=1, source_target_pairs={{0,8},{4,12},{8,16},{12,20},{16,24},{20,28},{24,0},{28,4},{1,9},{5... | collective-permute-start | bytes 1327112 | tf_op jit(solution)/shard_map/ppermute | solution.py:56
  171.2 22.4 %collective-permute-start.38 = (bf16[256,1792]{1,0:T(8,128)(2,1)S(1)}, bf16[256,1792]{1,0:T(8,128)(2,1)S(1)}, u32[]{:S(2)}, u32[]{:S(2)}) collective-permute-start(bf16[256,1792]{1,0:T(8,128)(2,1)S(1)} %fusion.2), channel_id=1, source_target_pairs={{0,4},{4,0},{8,12},{12,8},{16,20},{20,16},{24,28},{28,24},{1,5},{5... | collective-permute-start | bytes 2752520 | tf_op jit(solution)/shard_map/ppermute | solution.py:60
  182.1 4.1 %collective-permute-start.30 = (bf16[1,48,512]{2,1,0:T(8,128)(2,1)S(1)}, bf16[1,48,512]{2,1,0:T(8,128)(2,1)S(1)}, u32[]{:S(2)}, u32[]{:S(2)}) collective-permute-start(bf16[1,48,512]{2,1,0:T(8,128)(2,1)S(1)} %get-tuple-element.27), channel_id=1, source_target_pairs={{0,3},{1,2},{2,1},{3,0},{4,7},{5,6},{6,5},{7,4},{8,11},{9,10},{10,... | collective-permute-start | bytes 147464 | tf_op jit(solution)/shard_map/ppermute | solution.py:66
  182.2 5.7 %collective-permute-start.29 = (bf16[1,48,512]{2,1,0:T(8,128)(2,1)S(1)}, bf16[1,48,512]{2,1,0:T(8,128)(2,1)S(1)}, u32[]{:S(2)}, u32[]{:S(2)}) collective-permute-start(bf16[1,48,512]{2,1,0:T(8,128)(2,1)S(1)} %get-tuple-element.28), channel_id=1, source_target_pairs={{0,2},{1,3},{2,0},{3,1},{4,6},{5,7},{6,4},{7,5},{8,10},{9,11},{10,... | collective-permute-start | bytes 147464 | tf_op jit(solution)/shard_map/ppermute | solution.py:66
  183.6 4.4 %collective-permute-start.28 = (bf16[1,48,512]{2,1,0:T(8,128)(2,1)S(1)}, bf16[1,48,512]{2,1,0:T(8,128)(2,1)S(1)}, u32[]{:S(2)}, u32[]{:S(2)}) collective-permute-start(bf16[1,48,512]{2,1,0:T(8,128)(2,1)S(1)} %get-tuple-element.26), channel_id=1, source_target_pairs={{0,1},{1,0},{2,3},{3,2},{4,5},{5,4},{6,7},{7,6},{8,9},{9,8},{10,11... | collective-permute-start | bytes 147464 | tf_op jit(solution)/shard_map/ppermute | solution.py:66
  184.1 11.0 %collective-permute-start.25 = (bf16[48,512]{1,0:T(8,128)(2,1)S(1)}, bf16[48,512]{1,0:T(8,128)(2,1)S(1)}, u32[]{:S(2)}, u32[]{:S(2)}) collective-permute-start(bf16[48,512]{1,0:T(8,128)(2,1)S(1)} %get-tuple-element.40), channel_id=1, source_target_pairs={{0,8},{4,12},{8,16},{12,20},{16,24},{20,28},{24,0},{28,4},{1,9},{5... | collective-permute-start | bytes 147464 | tf_op jit(solution)/shard_map/ppermute | solution.py:56
  186.2 8.8 %collective-permute-start.32 = (bf16[48,512]{1,0:T(8,128)(2,1)S(1)}, bf16[48,512]{1,0:T(8,128)(2,1)S(1)}, u32[]{:S(2)}, u32[]{:S(2)}) collective-permute-start(bf16[48,512]{1,0:T(8,128)(2,1)S(1)} %get-tuple-element.39), channel_id=1, source_target_pairs={{0,24},{4,28},{8,0},{12,4},{16,8},{20,12},{24,16},{28,20},{1,25},{... | collective-permute-start | bytes 147464 | tf_op jit(solution)/shard_map/ppermute | solution.py:56
  188.0 7.1 %collective-permute-start.31 = (bf16[48,512]{1,0:T(8,128)(2,1)S(1)}, bf16[48,512]{1,0:T(8,128)(2,1)S(1)}, u32[]{:S(2)}, u32[]{:S(2)}) collective-permute-start(bf16[48,512]{1,0:T(8,128)(2,1)S(1)} %fusion.68), channel_id=1, source_target_pairs={{0,16},{4,20},{8,24},{12,28},{16,0},{20,4},{24,8},{28,12},{1,17},{... | collective-permute-start | bytes 147464 | tf_op jit(solution)/shard_map/ppermute | solution.py:56
  195.2 0.7 copy-start.5
